TPU v7x, 128 devices: a whole 4x4x4 slice. The times are simulated.
128 devices in a mesh: gz: 4 (over y), gy: 4 (over x_hi, core), gx: 8 (over z, x_lo).
Axes of the slice: x: 4 (x_hi: 2, x_lo: 2; x = x_hi * 2 + x_lo), y: 4, z: 4, core: 2. Of those that a mesh axis runs over, the one named last changes fastest.
Arguments:
- start: float32 [128, 64, 1024], P('gz', 'gy', 'gx'), may hold values from -21 to 21
- measured: float32 [128, 8, 1024], P(('gz', 'gy', 'gx')), may hold values from -18 to 18
- tiles: bfloat16 [8192, 8, 2048], P('gy', None, 'gx'), may hold values from -0.125 to 0.125
- tile_block: int32 [4, 8, 8], replicated, may hold values from 0 to 3
- angle_row: int32 [8], replicated, may hold values from 0 to 7, each once
Outputs:
- estimate: float32 [128, 64, 1024], P('gz', 'gy', 'gx')
- dual_state: float32 [3, 128, 64, 1024], P(None, 'gz', 'gy', 'gx')
Inputs may be any that keep to these rules, and one draw needn't show every extreme that they name: `tile_block`: which of the 4 detector blocks of 256 columns each brick's tile covers at each angle. `angle_row`: every row of measured is named once.
All inputs are finite; a program needn't handle non-finite values.
Results may differ from a plain program's by a relative error of at most 0.0008.
Values may be sent and summed in bfloat16 or wider, within the bound.
A program may use at most 128 MiB of HBM per device.

v0:
```python
import math

import jax
import jax.numpy as jnp
from jax import lax
from jax.experimental import pallas as pl
from jax.experimental.pallas import tpu as pltpu
from jax.sharding import PartitionSpec as P

CZ, CY, CX = 32, 16, 128
ROWS = CZ * CY
ANG, DW, NBLK = 8, 256, 4
V = CY * CX
R = 8
GZ, GY, GX = 4, 4, 8
BRICKS = GY * GX
CELLS = float(CZ * CY * CX * GZ * BRICKS)
MESH = pl.DeviceIdType.MESH
F32, BF16 = jnp.float32, jnp.bfloat16
STEP = 0.5
SHRINK = 0.2
EPS = 1e-6
CHUNK = 128
NCHUNK = V // CHUNK

RAW = [math.exp(-k * k / 12.5) for k in range(-R, R + 1)]
TAPS = [r / sum(RAW) for r in RAW]


def dot(a, b, dims):
    return lax.dot_general(a, b, (dims, ((), ())), preferred_element_type=F32)


def split(v):
    hi = v.astype(BF16)
    lo = (v - hi.astype(F32)).astype(BF16)
    return hi, lo


def kernel(
    start_ref, meas_ref, tiles_ref, tb_ref, row_ref,
    x_out, dual_out,
    raw, mat, tmp, vol, grad, xa, zbuf, ybuf, tbv, obs, mis,
    zs, zr, ys, yr, xs, xr,
    fzs, fzr, fys, fyr, fxs, fxr,
    stage, sl, snd1, rcv1, snd2, rcv2, rtmp,
    hterm, back, dl, dlm, xlr,
    red0, redz, red1, redx,
    bx, wx, acc,
    load_sem, tile_sem, hs_send, hs_recv, f_send, f_recv,
    a_send, a_recv, rz_send, rz_recv, rx_send, rx_recv, out_sem,
):
    gz, gy, gx = lax.axis_index("gz"), lax.axis_index("gy"), lax.axis_index("gx")
    me = gy * GX + gx

    ld = [
        pltpu.make_async_copy(start_ref, vol, load_sem.at[0]),
        pltpu.make_async_copy(meas_ref, obs, load_sem.at[1]),
    ]
    for c in ld:
        c.start()

    def tile_copy(c):
        rows = pl.ds(pl.multiple_of(c * CHUNK, CHUNK), CHUNK)
        return pltpu.make_async_copy(tiles_ref.at[rows], raw.at[rows], tile_sem.at[c])

    @pl.loop(0, NCHUNK)
    def _(c):
        tile_copy(c).start()

    barrier = pltpu.get_barrier_semaphore()

    def member(t):
        d = lax.rem(me + t, BRICKS)
        return d, (gz, d // GX, lax.rem(d, GX))

    @pl.loop(1, BRICKS)
    def _(t):
        pl.semaphore_signal(barrier, inc=1, device_id=member(t)[1], device_id_type=MESH)

    @pl.loop(1, GZ)
    def _(t):
        pl.semaphore_signal(
            barrier, inc=1, device_id=(lax.rem(gz + t, GZ), gy, gx), device_id_type=MESH
        )

    sides = {
        "z": (gz > 0, gz < GZ - 1, (gz - 1, gy, gx), (gz + 1, gy, gx)),
        "y": (gy > 0, gy < GY - 1, (gz, gy - 1, gx), (gz, gy + 1, gx)),
        "x": (gx > 0, gx < GX - 1, (gz, gy, gx - 1), (gz, gy, gx + 1)),
    }

    class Swap:
        def __init__(self, axis, src, dst, send, recv):
            self.has_lo, self.has_hi, low, high = sides[axis]
            self.lo = pltpu.make_async_remote_copy(
                src.at[0], dst.at[1], send.at[0], recv.at[1], device_id=low, device_id_type=MESH
            )
            self.hi = pltpu.make_async_remote_copy(
                src.at[1], dst.at[0], send.at[1], recv.at[0], device_id=high, device_id_type=MESH
            )
            self.dst = dst

        def clear(self):
            @pl.when(jnp.logical_not(self.has_lo))
            def _():
                self.dst[0] = jnp.zeros(self.dst.shape[1:], self.dst.dtype)

            @pl.when(jnp.logical_not(self.has_hi))
            def _():
                self.dst[1] = jnp.zeros(self.dst.shape[1:], self.dst.dtype)

        def start(self):
            @pl.when(self.has_lo)
            def _():
                self.lo.start()

            @pl.when(self.has_hi)
            def _():
                self.hi.start()

        def wait_recv(self):
            @pl.when(self.has_lo)
            def _():
                self.hi.wait_recv()

            @pl.when(self.has_hi)
            def _():
                self.lo.wait_recv()

        def wait_send(self):
            @pl.when(self.has_lo)
            def _():
                self.lo.wait_send()

            @pl.when(self.has_hi)
            def _():
                self.hi.wait_send()

    zsw = [Swap("z", zs.at[n], zr.at[n], hs_send.at[n, 0], hs_recv.at[n, 0]) for n in range(4)]
    ysw = [Swap("y", ys.at[n], yr.at[n], hs_send.at[n, 1], hs_recv.at[n, 1]) for n in range(4)]
    xsw = [Swap("x", xs.at[n], xr.at[n], hs_send.at[n, 2], hs_recv.at[n, 2]) for n in range(4)]
    fsw = [
        [
            Swap("z", fzs.at[n], fzr.at[n], f_send.at[n, 0], f_recv.at[n, 0]),
            Swap("y", fys.at[n], fyr.at[n], f_send.at[n, 1], f_recv.at[n, 1]),
            Swap("x", fxs.at[n], fxr.at[n], f_send.at[n, 2], f_recv.at[n, 2]),
        ]
        for n in range(3)
    ]
    every = zsw + ysw + xsw + [s for f in fsw for s in f]
    for s in every:
        s.clear()

    def gauss(d):
        df = d.astype(F32)
        w = jnp.exp(df * df * (-1.0 / 12.5)) * (1.0 / sum(RAW))
        return jnp.where(jnp.abs(d) <= R, w, 0.0)

    i0 = lax.broadcasted_iota(jnp.int32, (CX, CX), 0)
    i1 = lax.broadcasted_iota(jnp.int32, (CX, CX), 1)
    bhi, blo = split(gauss(i0 - i1))
    bx[0:CX] = bhi
    bx[CX : 2 * CX] = bhi
    bx[2 * CX : 3 * CX] = blo
    k0 = lax.broadcasted_iota(jnp.int32, (32, CX), 0)
    k1 = lax.broadcasted_iota(jnp.int32, (32, CX), 1)
    pos = jnp.where(k0 < 16, lax.rem(k0, 8) - 8, CX + lax.rem(k0, 8))
    whi, wlo = split(gauss(pos - k1))
    wx[0:32] = whi
    wx[32:64] = wlo
    rim = jnp.where(
        ((k1 == 0) & ((k0 == 7) | (k0 == 15))) | ((k1 == CX - 1) & ((k0 == 16) | (k0 == 24))),
        1.0,
        0.0,
    )
    wx[64:96] = rim.astype(BF16)
    s0 = lax.broadcasted_iota(jnp.int32, (32, 2 * CX), 0)
    s1 = lax.broadcasted_iota(jnp.int32, (32, 2 * CX), 1)
    want = jnp.where(s0 < 16, lax.rem(s0, 8), CX - 8 + lax.rem(s0, 8)) + jnp.where(
        lax.rem(s0, 16) < 8, 0, CX
    )
    pick = jnp.where(s1 == want, 1.0, 0.0).astype(BF16)

    e0 = lax.broadcasted_iota(jnp.int32, (GX, GX * CX), 0)
    e1 = lax.broadcasted_iota(jnp.int32, (GX, GX * CX), 1) // CX
    spread = jnp.where(e0 == e1, 1.0, 0.0).astype(BF16)
    for b in range(GY):
        rows = dot(tb_ref[b].astype(F32).astype(BF16), spread, ((0,), (0,)))
        for c in range(GX):
            tbv[b * GX + c] = rows[:, c * CX : (c + 1) * CX]

    for c in ld:
        c.wait()
    for a in range(ANG):
        acc[pl.ds(a, 1), :] = obs[0, pl.ds(row_ref[a], 1), :]

    pl.semaphore_wait(barrier, BRICKS - 1 + GZ - 1)

    def send_faces(n, src):
        fzs[n, 0] = src[0]
        fzs[n, 1] = src[CZ - 1]
        v = src[...]
        fys[n, 0] = v[:, 0, :]
        fys[n, 1] = v[:, CY - 1, :]
        hi, lo = split(v.reshape(ROWS, CX))
        f = dot(pick, jnp.concatenate([hi, lo], axis=1), ((1,), (1,))).astype(BF16)
        fxs[n, 0] = f[0:16]
        fxs[n, 1] = f[16:32]
        for s in fsw[n]:
            s.start()

    def send_z(n, src):
        zs[n, 0] = src[0:R].reshape(R * CY, CX).astype(BF16)
        zs[n, 1] = src[CZ - R : CZ].reshape(R * CY, CX).astype(BF16)
        zsw[n].start()

    def blur(n, src, between):
        zbuf[R : R + CZ] = src[...]
        between()
        zsw[n].wait_recv()
        zbuf[0:R] = zr[n, 0].astype(F32).reshape(R, CY, CX)
        zbuf[R + CZ :] = zr[n, 1].astype(F32).reshape(R, CY, CX)

        @pl.loop(0, CZ)
        def _(z):
            t = TAPS[R] * zbuf[z + R]
            for k in range(R):
                t += TAPS[k] * (zbuf[z + k] + zbuf[z + 2 * R - k])
            ybuf[z, R : R + CY, :] = t

        ys[n, 0] = ybuf[:, R : 2 * R, :].reshape(CZ * R, CX).astype(BF16)
        ys[n, 1] = ybuf[:, CY : R + CY, :].reshape(CZ * R, CX).astype(BF16)
        ysw[n].start()
        ysw[n].wait_recv()
        ybuf[:, 0:R, :] = yr[n, 0].astype(F32).reshape(CZ, R, CX)
        ybuf[:, R + CY :, :] = yr[n, 1].astype(F32).reshape(CZ, R, CX)

        @pl.loop(0, CZ)
        def _(z):
            t = TAPS[R] * ybuf[z, R : R + CY, :]
            for k in range(R):
                t += TAPS[k] * (ybuf[z, k : k + CY, :] + ybuf[z, 2 * R - k : 2 * R - k + CY, :])
            grad[pl.ds(pl.multiple_of(z * CY, CY), CY), :] = t

        hi, lo = split(grad[...])
        both = jnp.concatenate([hi, lo], axis=1)
        f = dot(pick, both, ((1,), (1,))).astype(BF16)
        xs[n, 0] = f[0:16]
        xs[n, 1] = f[16:32]
        xsw[n].start()
        own = dot(both, bx[0 : 2 * CX], ((1,), (0,))) + dot(hi, bx[2 * CX :], ((1,), (0,)))
        xsw[n].wait_recv()
        halo = xr[n].reshape(32, ROWS)
        return own + dot(halo, wx[0:32], ((0,), (0,))) + dot(halo, wx[32:64], ((0,), (0,)))

    lane = lax.broadcasted_iota(jnp.int32, (CY, CX), 1)
    sub = lax.broadcasted_iota(jnp.int32, (CY, CX), 0)
    first = {
        "z": (gz == 0, gz == GZ - 1),
        "y": (gy == 0, gy == GY - 1),
        "x": (gx == 0, gx == GX - 1),
    }

    def wait_faces(n):
        for s in fsw[n]:
            s.wait_recv()
        xlr[...] = dot(fxr[n].reshape(32, ROWS), wx[64:96], ((0,), (0,))).reshape(CZ, CY, CX)
        xa[0] = fzr[n, 0]
        xa[CZ + 1] = fzr[n, 1]

    def diffs(n, z):
        v = xa[z + 1]
        out = []
        up, low = xa[z + 2], xa[z]
        out.append((
            jnp.where((z == CZ - 1) & first["z"][1], 0.0, up - v),
            jnp.where((z == 0) & first["z"][0], 0.0, v - low),
        ))
        rim = fyr[n, 1, pl.ds(z, 1), :]
        up = jnp.where(sub == CY - 1, rim, pltpu.roll(v, CY - 1, 0))
        rim = fyr[n, 0, pl.ds(z, 1), :]
        low = jnp.where(sub == 0, rim, pltpu.roll(v, 1, 0))
        out.append((
            jnp.where((sub == CY - 1) & first["y"][1], 0.0, up - v),
            jnp.where((sub == 0) & first["y"][0], 0.0, v - low),
        ))
        edge = xlr[z]
        up = jnp.where(lane == CX - 1, edge, pltpu.roll(v, CX - 1, 1))
        low = jnp.where(lane == 0, edge, pltpu.roll(v, 1, 1))
        out.append((
            jnp.where((lane == CX - 1) & first["x"][1], 0.0, up - v),
            jnp.where((lane == 0) & first["x"][0], 0.0, v - low),
        ))
        return out

    def fold(p):
        return p[0:8] + p[8:16]

    def send_sums(n, primal, dualres):
        p = jnp.sum(primal, axis=0, keepdims=True)
        d = jnp.sum(dualres, axis=0, keepdims=True)
        r8 = lax.broadcasted_iota(jnp.int32, (8, CX), 0)
        red0[n] = jnp.where(r8 < 4, p, d)

        for t in range(1, GZ):
            redz_copy(n, t).start()

    def redz_copy(n, t):
        return pltpu.make_async_remote_copy(
            red0.at[n], redz.at[n, t], rz_send.at[n, t], rz_recv.at[n, t],
            device_id=(lax.rem(gz + t, GZ), gy, gx), device_id_type=MESH,
        )

    def redx_copy(n, t):
        return pltpu.make_async_remote_copy(
            red1.at[n], redx.at[n, t], rx_send.at[n], rx_recv.at[n],
            device_id=member(t)[1], device_id_type=MESH,
        )

    def forward_sums(n):
        total = red0[n]
        for t in range(1, GZ):
            redz_copy(n, t).wait_recv()
            total += redz[n, t]
        red1[n] = total

        @pl.loop(1, BRICKS)
        def _(t):
            redx_copy(n, t).start()

    def finish_sums(n):
        total = red1[n]
        got = redx.at[n, pl.ds(1, BRICKS - 1)]
        pltpu.make_async_copy(got, got, rx_recv.at[n]).wait()
        total += jnp.sum(redx[n, 1:BRICKS], axis=0)
        p = jnp.sum(total[0:1], axis=1, keepdims=True)
        d = jnp.sum(total[4:5], axis=1, keepdims=True)
        return jnp.broadcast_to(p, (8, CX)), jnp.broadcast_to(d, (8, CX))

    send_z(0, vol)
    send_faces(0, vol)

    def relayout():
        @pl.loop(0, NCHUNK)
        def _(c):
            tile_copy(c).wait()
            rows = pl.ds(pl.multiple_of(c * CHUNK, CHUNK), CHUNK)
            block = raw[rows].astype(F32).reshape(CHUNK * ANG, DW)
            for h in range(2):
                tmp[h] = block[:, h * 128 : (h + 1) * 128]
            for a in range(ANG):
                for h in range(2):
                    part = tmp[h, pl.ds(a, CHUNK, stride=ANG), :]
                    mat[rows, a * DW + h * 128 : a * DW + (h + 1) * 128] = part.astype(BF16)

    def first_terms():
        wait_faces(0)
        xa[1 : CZ + 1] = vol[...]
        cut = SHRINK

        @pl.loop(0, CZ)
        def _(z):
            smooth = jnp.zeros((CY, CX), F32)
            shrunk = jnp.zeros((CY, CX), F32)
            for j, jm in diffs(0, z):
                s = j - jnp.clip(j, -cut, cut)
                sm = jm - jnp.clip(jm, -cut, cut)
                smooth += jm - j
                shrunk += sm - s
            hterm[z] = smooth - shrunk
            back[z] = shrunk

    def copy1(n, d, dev):
        return pltpu.make_async_remote_copy(
            snd1.at[n, d], rcv1.at[n, me], a_send.at[n, 0], a_recv.at[n, 0],
            device_id=dev, device_id_type=MESH,
        )

    def copy2(n, d, dev):
        return pltpu.make_async_remote_copy(
            snd2.at[n, d], rcv2.at[n, me], a_send.at[n, 1], a_recv.at[n, 1],
            device_id=dev, device_id_type=MESH,
        )

    def arrivals(ref, sem):
        got = ref.at[pl.ds(0, BRICKS - 1)]
        pltpu.make_async_copy(got, got, sem).wait()

    def project(n, blurred, between):
        grad[...] = blurred
        for y in range(CY):
            sl[:, y * CX : (y + 1) * CX] = grad[pl.ds(y, CZ, stride=CY), :].astype(BF16)
        for a in range(ANG):
            c = dot(sl[...], mat[:, a * DW : (a + 1) * DW], ((1,), (0,)))
            for h in range(2):
                stage[h, pl.ds(a, CZ, stride=ANG), :] = c[:, h * 128 : (h + 1) * 128]

        def block_of(d):
            rows = pl.ds(pl.multiple_of(d * ANG, ANG), ANG)
            return jnp.concatenate([stage[0, rows, :], stage[1, rows, :]], axis=1).astype(BF16)

        @pl.loop(1, BRICKS)
        def _(t):
            d, dev = member(t)
            snd1[n, d] = block_of(d)
            copy1(n, d, dev).start()

        rcv1[n, me] = block_of(me)
        between()
        arrivals(rcv1.at[n], a_recv.at[n, 0])

        def add(s, sums):
            x = rcv1[n, s].astype(F32)
            t = tbv[s]
            t = jnp.concatenate([t, t], axis=1)
            return tuple(sums[q] + jnp.where(t == float(q), x, 0.0) for q in range(NBLK))

        sums = lax.fori_loop(
            0, BRICKS, add, tuple(jnp.zeros((ANG, DW), F32) for _ in range(NBLK))
        )
        for q in range(NBLK):
            cols = slice(q * DW, (q + 1) * DW)
            mis[:, cols] = (sums[q] - acc[:, cols]).astype(BF16).astype(F32)

        def chosen(d):
            t = tbv[d]
            t = jnp.concatenate([t, t], axis=1)
            c = mis[:, 0:DW]
            for q in range(1, NBLK):
                c = jnp.where(t == float(q), mis[:, q * DW : (q + 1) * DW], c)
            return c.astype(BF16)

        @pl.loop(1, BRICKS)
        def _(t):
            d, dev = member(t)
            snd2[n, d] = chosen(d)
            copy2(n, d, dev).start()

        rcv2[n, me] = chosen(me)

    def backproject(n):
        arrivals(rcv2.at[n], a_recv.at[n, 1])
        r = rcv2[n].astype(F32).reshape(CZ * ANG, DW)
        for h in range(2):
            stage[h] = r[:, h * 128 : (h + 1) * 128]
        for a in range(ANG):
            for h in range(2):
                sl[:, a * DW + h * 128 : a * DW + (h + 1) * 128] = stage[
                    h, pl.ds(a, CZ, stride=ANG), :
                ].astype(BF16)
        for c in range(ANG):
            b = dot(sl[...], mat[c * DW : (c + 1) * DW, :], ((1,), (1,)))
            for h in range(2):
                grad[pl.ds(2 * c + h, CZ, stride=CY), :] = b[:, h * 128 : (h + 1) * 128]

    def before():
        first_terms()
        relayout()

    project(0, blur(0, vol, before), lambda: None)
    backproject(0)
    vol[...] = grad[...].reshape(CZ, CY, CX)
    send_z(1, vol)
    g = blur(1, vol, lambda: None).reshape(CZ, CY, CX)
    xa[1 : CZ + 1] = xa[1 : CZ + 1] - STEP * (g + hterm[...])
    vol[...] = xa[1 : CZ + 1]
    send_z(2, vol)
    send_faces(1, vol)

    def second_terms():
        wait_faces(1)
        cut = SHRINK

        def one(z, sums):
            primal, dres = sums
            smooth = jnp.zeros((CY, CX), F32)
            shrunk = jnp.zeros((CY, CX), F32)
            bdual = jnp.zeros((CY, CX), F32)
            for axis, (j, jm) in enumerate(diffs(1, z)):
                d = jnp.clip(j, -cut, cut)
                dm = jnp.clip(jm, -cut, cut)
                s = j - d
                sm = jm - dm
                d = j - s
                dm = jm - sm
                smooth += jm - j
                shrunk += sm - s
                bdual += dm - d
                dl[axis, z] = d
                dlm[axis, z] = dm
                primal += fold(jnp.square(j - s))
            dres += fold(jnp.square(shrunk - back[z]))
            hterm[z] = smooth - shrunk
            back[z] = shrunk
            zbuf[z] = bdual
            return primal, dres

        zero = jnp.zeros((8, CX), F32)
        primal, dres = lax.fori_loop(0, CZ, one, (zero, zero))
        send_sums(0, primal, dres)

    def factor_of(n, penalty):
        p, d = finish_sums(n)
        p = p * (1.0 / (3.0 * CELLS))
        d = penalty * penalty * d * (1.0 / CELLS)
        return jnp.sqrt(jnp.sqrt((p + EPS) / (d + EPS)))

    def keep_terms():
        second_terms()

    blurred = blur(2, vol, lambda: None)
    keep_terms()
    bd = zbuf[0:CZ]
    dual_keep = bd
    xlr[...] = dual_keep

    def pass_sums():
        forward_sums(0)

    project(1, blurred, pass_sums)
    factor1 = factor_of(0, jnp.ones((8, CX), F32))
    penalty = factor1
    inv1 = 1.0 / factor1
    pen3 = penalty[0:1].reshape(1, 1, CX)
    inv3 = inv1[0:1].reshape(1, 1, CX)
    hterm[...] = STEP * pen3 * (hterm[...] + xlr[...] * inv3)
    backproject(1)
    vol[...] = grad[...].reshape(CZ, CY, CX)
    send_z(3, vol)
    g = blur(3, vol, lambda: None).reshape(CZ, CY, CX)
    xa[1 : CZ + 1] = xa[1 : CZ + 1] - (STEP * g + hterm[...])
    vol[...] = xa[1 : CZ + 1]
    send_faces(2, vol)
    x_copy = pltpu.make_async_copy(vol, x_out, out_sem.at[0])
    x_copy.start()

    wait_faces(2)
    cut = (SHRINK / penalty)[0:1]
    inv = inv1[0:1]

    def last(z, sums):
        primal, dres = sums
        shrunk = jnp.zeros((CY, CX), F32)
        for axis, (j, jm) in enumerate(diffs(2, z)):
            t = j + dl[axis, z] * inv
            tm = jm + dlm[axis, z] * inv
            s = t - jnp.clip(t, -cut, cut)
            sm = tm - jnp.clip(tm, -cut, cut)
            shrunk += sm - s
            dl[axis, z] = t - s
            primal += fold(jnp.square(j - s))
        dres += fold(jnp.square(shrunk - back[z]))
        return primal, dres

    zero = jnp.zeros((8, CX), F32)
    primal, dres = lax.fori_loop(0, CZ, last, (zero, zero))
    send_sums(1, primal, dres)
    forward_sums(1)
    factor2 = factor_of(1, penalty)
    scale = (1.0 / factor2)[0:1].reshape(1, 1, 1, CX)
    dl[...] = dl[...] * scale
    d_copy = pltpu.make_async_copy(dl, dual_out, out_sem.at[1])
    d_copy.start()

    for s in every:
        s.wait_send()
    for n in range(2):
        for i, ref in enumerate((snd1, snd2)):
            arrivals(ref.at[n], a_send.at[n, i])
        for t in range(1, GZ):
            redz_copy(n, t).wait_send()
        got = redx.at[n, pl.ds(1, BRICKS - 1)]
        pltpu.make_async_copy(got, got, rx_send.at[n]).wait()
    x_copy.wait()
    d_copy.wait()


def body(start, measured, tiles, tile_block, angle_row):
    vm = pltpu.VMEM
    dma = pltpu.SemaphoreType.DMA
    return pl.pallas_call(
        kernel,
        out_shape=(
            jax.ShapeDtypeStruct((CZ, CY, CX), F32),
            jax.ShapeDtypeStruct((3, CZ, CY, CX), F32),
        ),
        in_specs=[
            pl.BlockSpec(memory_space=pl.ANY),
            pl.BlockSpec(memory_space=pl.ANY),
            pl.BlockSpec(memory_space=pl.ANY),
            pl.BlockSpec(memory_space=pltpu.VMEM),
            pl.BlockSpec(memory_space=pltpu.SMEM),
        ],
        out_specs=(pl.BlockSpec(memory_space=pl.ANY), pl.BlockSpec(memory_space=pl.ANY)),
        scratch_shapes=[
            vm((V, ANG, DW), BF16),
            vm((V, ANG * DW), BF16),
            vm((2, CHUNK * ANG, 128), F32),
            vm((CZ, CY, CX), F32),
            vm((ROWS, CX), F32),
            vm((CZ + 2, CY, CX), F32),
            vm((CZ + 2 * R, CY, CX), F32),
            vm((CZ, CY + 2 * R, CX), F32),
            vm((BRICKS, ANG, CX), F32),
            vm((1, ANG, NBLK * DW), F32),
            vm((ANG, NBLK * DW), F32),
            vm((4, 2, R * CY, CX), BF16),
            vm((4, 2, R * CY, CX), BF16),
            vm((4, 2, CZ * R, CX), BF16),
            vm((4, 2, CZ * R, CX), BF16),
            vm((4, 2, 16, ROWS), BF16),
            vm((4, 2, 16, ROWS), BF16),
            vm((3, 2, CY, CX), F32),
            vm((3, 2, CY, CX), F32),
            vm((3, 2, CZ, CX), F32),
            vm((3, 2, CZ, CX), F32),
            vm((3, 2, 16, ROWS), BF16),
            vm((3, 2, 16, ROWS), BF16),
            vm((2, CZ * ANG, 128), F32),
            vm((CZ, V), BF16),
            vm((2, BRICKS, ANG, DW), BF16),
            vm((2, BRICKS, ANG, DW), BF16),
            vm((2, BRICKS, ANG, DW), BF16),
            vm((2, BRICKS, ANG, DW), BF16),
            vm((8, CX), F32),
            vm((CZ, CY, CX), F32),
            vm((CZ, CY, CX), F32),
            vm((3, CZ, CY, CX), F32),
            vm((3, CZ, CY, CX), F32),
            vm((CZ, CY, CX), F32),
            vm((2, 8, CX), F32),
            vm((2, GZ, 8, CX), F32),
            vm((2, 8, CX), F32),
            vm((2, BRICKS, 8, CX), F32),
            vm((3 * CX, CX), BF16),
            vm((96, CX), BF16),
            vm((ANG, NBLK * DW), F32),
            dma((2,)),
            dma((NCHUNK,)),
            dma((4, 3, 2)),
            dma((4, 3, 2)),
            dma((3, 3, 2)),
            dma((3, 3, 2)),
            dma((2, 2)),
            dma((2, 2)),
            dma((2, GZ)),
            dma((2, GZ)),
            dma((2,)),
            dma((2,)),
            dma((2,)),
        ],
        compiler_params=pltpu.CompilerParams(
            collective_id=0, has_side_effects=True, vmem_limit_bytes=60 * 1024 * 1024
        ),
    )(start, measured, tiles, tile_block, angle_row)


def solution(mesh):
    return jax.shard_map(
        body,
        mesh=mesh,
        in_specs=(
            P("gz", "gy", "gx"),
            P(("gz", "gy", "gx"), None, None),
            P("gy", None, "gx"),
            P(),
            P(),
        ),
        out_specs=(P("gz", "gy", "gx"), P(None, "gz", "gy", "gx")),
        check_vma=False,
    )
```

profile of v0, /device:TPU:1, one launch (start us, length us, event | category | flops | bytes accessed | tf_op | source)
XLA Modules:
  0.0 115.0 jit_solution(14498297795379793077)
XLA Ops:
  0.6 110.6 %shard_map.68 = (f32[32,16,128]{2,1,0:T(8,128)}, f32[3,32,16,128]{3,2,1,0:T(8,128)}) custom-call(f32[32,16,128]{2,1,0:T(8,128)} %start_ref.1, f32[1,8,1024]{2,1,0:T(8,128)} %meas_ref.1, bf16[2048,8,256]{2,1,0:T(8,128)(2,1)} %tiles_ref.1, s32[4,8,8]{2,1,0:T(8,128)} %tb_ref.1, s32[8]{0:T(128)} %row_ref.1), custom_call_target="tpu_custom_call" | custom-call | tf_op jit(solution)/shard_map/pallas_call | solution.py:582
  111.3 1.7 %copy.9 = f32[32,16,128]{2,1,0:T(8,128)} copy(f32[32,16,128]{2,1,0:T(8,128)} %get-tuple-element.4) | data formatting | bytes 524288
  112.9 2.1 %copy.10 = f32[3,32,16,128]{3,2,1,0:T(8,128)} copy(f32[3,32,16,128]{3,2,1,0:T(8,128)} %get-tuple-element.5) | data formatting | bytes 1572864
where the time goes:
time: 115 us
  Pallas kernels  111 us (97%)
  local copies, waits for them, and re-layouts  3.73 us (3%)
    pallas_call x1, Pallas kernels, body(): pl.pallas_call(kernel, out_shape=(jax.ShapeDtypeStruct((CZ, CY, CX), F32)...  111 us
    unnamed x2, local copies, waits for them, and re-layouts  3.73 us

commit v1 on v0

--- a/solution.py
+++ b/solution.py
@@ -43,7 +43,7 @@
     raw, mat, tmp, vol, grad, xa, zbuf, ybuf, tbv, obs, mis,
     zs, zr, ys, yr, xs, xr,
     fzs, fzr, fys, fyr, fxs, fxr,
-    stage, sl, snd1, rcv1, snd2, rcv2, rtmp,
+    stage, sl, snd1, rcv1, snd2, rcv2, rmis,
     hterm, back, dl, dlm, xlr,
     red0, redz, red1, redx,
     bx, wx, acc,
@@ -190,12 +190,27 @@
         for c in range(GX):
             tbv[b * GX + c] = rows[:, c * CX : (c + 1) * CX]
 
+    def relayout(low, high):
+        @pl.loop(low, high)
+        def _(c):
+            tile_copy(c).wait()
+            rows = pl.ds(pl.multiple_of(c * CHUNK, CHUNK), CHUNK)
+            block = raw[rows].astype(F32).reshape(CHUNK * ANG, DW)
+            for h in range(2):
+                tmp[h] = block[:, h * 128 : (h + 1) * 128]
+            for a in range(ANG):
+                for h in range(2):
+                    part = tmp[h, pl.ds(a, CHUNK, stride=ANG), :]
+                    mat[rows, a * DW + h * 128 : a * DW + (h + 1) * 128] = part.astype(BF16)
+
     for c in ld:
         c.wait()
     for a in range(ANG):
         acc[pl.ds(a, 1), :] = obs[0, pl.ds(row_ref[a], 1), :]
 
-    pl.semaphore_wait(barrier, BRICKS - 1 + GZ - 1)
+    relayout(0, 6)
+    with jax.named_scope("wait_barrier"):
+        pl.semaphore_wait(barrier, BRICKS - 1 + GZ - 1)
 
     def send_faces(n, src):
         fzs[n, 0] = src[0]
@@ -210,15 +225,19 @@
         for s in fsw[n]:
             s.start()
 
+    def nothing():
+        pass
+
     def send_z(n, src):
         zs[n, 0] = src[0:R].reshape(R * CY, CX).astype(BF16)
         zs[n, 1] = src[CZ - R : CZ].reshape(R * CY, CX).astype(BF16)
         zsw[n].start()
 
-    def blur(n, src, between):
+    def blur(n, src, between=nothing, in_y=nothing, in_x=nothing):
         zbuf[R : R + CZ] = src[...]
         between()
-        zsw[n].wait_recv()
+        with jax.named_scope("wait_z"):
+            zsw[n].wait_recv()
         zbuf[0:R] = zr[n, 0].astype(F32).reshape(R, CY, CX)
         zbuf[R + CZ :] = zr[n, 1].astype(F32).reshape(R, CY, CX)
 
@@ -232,7 +251,9 @@
         ys[n, 0] = ybuf[:, R : 2 * R, :].reshape(CZ * R, CX).astype(BF16)
         ys[n, 1] = ybuf[:, CY : R + CY, :].reshape(CZ * R, CX).astype(BF16)
         ysw[n].start()
-        ysw[n].wait_recv()
+        in_y()
+        with jax.named_scope("wait_y"):
+            ysw[n].wait_recv()
         ybuf[:, 0:R, :] = yr[n, 0].astype(F32).reshape(CZ, R, CX)
         ybuf[:, R + CY :, :] = yr[n, 1].astype(F32).reshape(CZ, R, CX)
 
@@ -250,7 +271,9 @@
         xs[n, 1] = f[16:32]
         xsw[n].start()
         own = dot(both, bx[0 : 2 * CX], ((1,), (0,))) + dot(hi, bx[2 * CX :], ((1,), (0,)))
-        xsw[n].wait_recv()
+        in_x()
+        with jax.named_scope("wait_x"):
+            xsw[n].wait_recv()
         halo = xr[n].reshape(32, ROWS)
         return own + dot(halo, wx[0:32], ((0,), (0,))) + dot(halo, wx[32:64], ((0,), (0,)))
 
@@ -298,10 +321,9 @@
         return p[0:8] + p[8:16]
 
     def send_sums(n, primal, dualres):
-        p = jnp.sum(primal, axis=0, keepdims=True)
-        d = jnp.sum(dualres, axis=0, keepdims=True)
-        r8 = lax.broadcasted_iota(jnp.int32, (8, CX), 0)
-        red0[n] = jnp.where(r8 < 4, p, d)
+        p = jnp.sum(jnp.sum(primal, axis=0, keepdims=True), axis=1, keepdims=True)
+        d = jnp.sum(jnp.sum(dualres, axis=0, keepdims=True), axis=1, keepdims=True)
+        red0[n] = jnp.where(lane[0:1] < CX // 2, p, d)
 
         for t in range(1, GZ):
             redz_copy(n, t).start()
@@ -334,28 +356,15 @@
         got = redx.at[n, pl.ds(1, BRICKS - 1)]
         pltpu.make_async_copy(got, got, rx_recv.at[n]).wait()
         total += jnp.sum(redx[n, 1:BRICKS], axis=0)
-        p = jnp.sum(total[0:1], axis=1, keepdims=True)
-        d = jnp.sum(total[4:5], axis=1, keepdims=True)
+        p, d = total[:, 0:1], total[:, CX - 1 : CX]
         return jnp.broadcast_to(p, (8, CX)), jnp.broadcast_to(d, (8, CX))
 
     send_z(0, vol)
     send_faces(0, vol)
 
-    def relayout():
-        @pl.loop(0, NCHUNK)
-        def _(c):
-            tile_copy(c).wait()
-            rows = pl.ds(pl.multiple_of(c * CHUNK, CHUNK), CHUNK)
-            block = raw[rows].astype(F32).reshape(CHUNK * ANG, DW)
-            for h in range(2):
-                tmp[h] = block[:, h * 128 : (h + 1) * 128]
-            for a in range(ANG):
-                for h in range(2):
-                    part = tmp[h, pl.ds(a, CHUNK, stride=ANG), :]
-                    mat[rows, a * DW + h * 128 : a * DW + (h + 1) * 128] = part.astype(BF16)
-
     def first_terms():
-        wait_faces(0)
+        with jax.named_scope("first_terms"):
+            wait_faces(0)
         xa[1 : CZ + 1] = vol[...]
         cut = SHRINK
 
@@ -391,7 +400,8 @@
         grad[...] = blurred
         for y in range(CY):
             sl[:, y * CX : (y + 1) * CX] = grad[pl.ds(y, CZ, stride=CY), :].astype(BF16)
-        for a in range(ANG):
+        with jax.named_scope("mm_fwd"):
+          for a in range(ANG):
             c = dot(sl[...], mat[:, a * DW : (a + 1) * DW], ((1,), (0,)))
             for h in range(2):
                 stage[h, pl.ds(a, CZ, stride=ANG), :] = c[:, h * 128 : (h + 1) * 128]
@@ -408,7 +418,8 @@
 
         rcv1[n, me] = block_of(me)
         between()
-        arrivals(rcv1.at[n], a_recv.at[n, 0])
+        with jax.named_scope("wait_a1"):
+            arrivals(rcv1.at[n], a_recv.at[n, 0])
 
         def add(s, sums):
             x = rcv1[n, s].astype(F32)
@@ -440,7 +451,8 @@
         rcv2[n, me] = chosen(me)
 
     def backproject(n):
-        arrivals(rcv2.at[n], a_recv.at[n, 1])
+        with jax.named_scope("wait_a2"):
+            arrivals(rcv2.at[n], a_recv.at[n, 1])
         r = rcv2[n].astype(F32).reshape(CZ * ANG, DW)
         for h in range(2):
             stage[h] = r[:, h * 128 : (h + 1) * 128]
@@ -449,27 +461,26 @@
                 sl[:, a * DW + h * 128 : a * DW + (h + 1) * 128] = stage[
                     h, pl.ds(a, CZ, stride=ANG), :
                 ].astype(BF16)
-        for c in range(ANG):
+        with jax.named_scope("mm_bwd"):
+          for c in range(ANG):
             b = dot(sl[...], mat[c * DW : (c + 1) * DW, :], ((1,), (1,)))
             for h in range(2):
                 grad[pl.ds(2 * c + h, CZ, stride=CY), :] = b[:, h * 128 : (h + 1) * 128]
 
-    def before():
-        first_terms()
-        relayout()
-
-    project(0, blur(0, vol, before), lambda: None)
+    blurred = blur(0, vol, lambda: relayout(6, 12), lambda: relayout(12, NCHUNK))
+    project(0, blurred, first_terms)
     backproject(0)
     vol[...] = grad[...].reshape(CZ, CY, CX)
     send_z(1, vol)
-    g = blur(1, vol, lambda: None).reshape(CZ, CY, CX)
+    g = blur(1, vol).reshape(CZ, CY, CX)
     xa[1 : CZ + 1] = xa[1 : CZ + 1] - STEP * (g + hterm[...])
     vol[...] = xa[1 : CZ + 1]
     send_z(2, vol)
     send_faces(1, vol)
 
     def second_terms():
-        wait_faces(1)
+        with jax.named_scope("second_terms"):
+            wait_faces(1)
         cut = SHRINK
 
         def one(z, sums):
@@ -493,7 +504,7 @@
             dres += fold(jnp.square(shrunk - back[z]))
             hterm[z] = smooth - shrunk
             back[z] = shrunk
-            zbuf[z] = bdual
+            xlr[z] = bdual
             return primal, dres
 
         zero = jnp.zeros((8, CX), F32)
@@ -506,36 +517,30 @@
         d = penalty * penalty * d * (1.0 / CELLS)
         return jnp.sqrt(jnp.sqrt((p + EPS) / (d + EPS)))
 
-    def keep_terms():
-        second_terms()
-
-    blurred = blur(2, vol, lambda: None)
-    keep_terms()
-    bd = zbuf[0:CZ]
-    dual_keep = bd
-    xlr[...] = dual_keep
-
-    def pass_sums():
-        forward_sums(0)
-
-    project(1, blurred, pass_sums)
-    factor1 = factor_of(0, jnp.ones((8, CX), F32))
-    penalty = factor1
-    inv1 = 1.0 / factor1
-    pen3 = penalty[0:1].reshape(1, 1, CX)
-    inv3 = inv1[0:1].reshape(1, 1, CX)
-    hterm[...] = STEP * pen3 * (hterm[...] + xlr[...] * inv3)
+    project(1, blur(2, vol), second_terms)
+    forward_sums(0)
     backproject(1)
+    ones = jnp.ones((8, CX), F32)
+
+    def new_penalty():
+        factor = factor_of(0, ones)
+        pen3 = factor[0:1].reshape(1, 1, CX)
+        hterm[...] = STEP * pen3 * (hterm[...] + xlr[...] * (1.0 / pen3))
+        rmis[...] = factor
+
     vol[...] = grad[...].reshape(CZ, CY, CX)
     send_z(3, vol)
-    g = blur(3, vol, lambda: None).reshape(CZ, CY, CX)
+    g = blur(3, vol, new_penalty).reshape(CZ, CY, CX)
+    penalty = rmis[...]
+    inv1 = 1.0 / penalty
     xa[1 : CZ + 1] = xa[1 : CZ + 1] - (STEP * g + hterm[...])
     vol[...] = xa[1 : CZ + 1]
     send_faces(2, vol)
     x_copy = pltpu.make_async_copy(vol, x_out, out_sem.at[0])
     x_copy.start()
 
-    wait_faces(2)
+    with jax.named_scope("wait_faces"):
+        wait_faces(2)
     cut = (SHRINK / penalty)[0:1]
     inv = inv1[0:1]
 
@@ -556,14 +561,17 @@
     zero = jnp.zeros((8, CX), F32)
     primal, dres = lax.fori_loop(0, CZ, last, (zero, zero))
     send_sums(1, primal, dres)
-    forward_sums(1)
-    factor2 = factor_of(1, penalty)
+    with jax.named_scope("sums_z"):
+        forward_sums(1)
+    with jax.named_scope("sums_x"):
+        factor2 = factor_of(1, penalty)
     scale = (1.0 / factor2)[0:1].reshape(1, 1, 1, CX)
     dl[...] = dl[...] * scale
     d_copy = pltpu.make_async_copy(dl, dual_out, out_sem.at[1])
     d_copy.start()
 
-    for s in every:
+    with jax.named_scope("wait_sends"):
+      for s in every:
         s.wait_send()
     for n in range(2):
         for i, ref in enumerate((snd1, snd2)):
@@ -629,10 +637,10 @@
             vm((3, CZ, CY, CX), F32),
             vm((3, CZ, CY, CX), F32),
             vm((CZ, CY, CX), F32),
-            vm((2, 8, CX), F32),
-            vm((2, GZ, 8, CX), F32),
-            vm((2, 8, CX), F32),
-            vm((2, BRICKS, 8, CX), F32),
+            vm((2, 1, CX), F32),
+            vm((2, GZ, 1, CX), F32),
+            vm((2, 1, CX), F32),
+            vm((2, BRICKS, 1, CX), F32),
             vm((3 * CX, CX), BF16),
             vm((96, CX), BF16),
             vm((ANG, NBLK * DW), F32),

time: 115 us -> 104 us (0.904)
  Pallas kernels: 111 us -> 99.1 us
    pallas_call x1, Pallas kernels: 111 us -> 99.1 us  [body(): pl.pallas_call(kernel, out_shape=(jax.ShapeDtypeStruct((CZ, CY, CX), F32)...]
where the time goes in v1:
time: 104 us; the launch traced here: 103 us
  Pallas kernels  99.1 us (95%)
  local copies, waits for them, and re-layouts  3.73 us (4%)
    pallas_call x1, Pallas kernels, body(): pl.pallas_call(kernel, out_shape=(jax.ShapeDtypeStruct((CZ, CY, CX), F32)...  99.1 us
    unnamed x2, local copies, waits for them, and re-layouts  3.73 us

profile of v1, /device:TPU:1, one launch (start us, length us, event | category | flops | bytes accessed | tf_op | source)
XLA Modules:
  0.0 103.5 jit_solution(9707493527034839397)
XLA Ops:
  0.6 99.1 %shard_map.68 = (f32[32,16,128]{2,1,0:T(8,128)}, f32[3,32,16,128]{3,2,1,0:T(8,128)}) custom-call(f32[32,16,128]{2,1,0:T(8,128)} %start_ref.1, f32[1,8,1024]{2,1,0:T(8,128)} %meas_ref.1, bf16[2048,8,256]{2,1,0:T(8,128)(2,1)} %tiles_ref.1, s32[4,8,8]{2,1,0:T(8,128)} %tb_ref.1, s32[8]{0:T(128)} %row_ref.1), custom_call_target="tpu_custom_call" | custom-call | tf_op jit(solution)/shard_map/pallas_call | solution.py:590
  99.7 1.7 %copy.9 = f32[32,16,128]{2,1,0:T(8,128)} copy(f32[32,16,128]{2,1,0:T(8,128)} %get-tuple-element.4) | data formatting | bytes 524288
  101.4 2.1 %copy.10 = f32[3,32,16,128]{3,2,1,0:T(8,128)} copy(f32[3,32,16,128]{3,2,1,0:T(8,128)} %get-tuple-element.5) | data formatting | bytes 1572864

commit v2 on v1

v2 whole, which is shorter than its diff:
```python
import math

import jax
import jax.numpy as jnp
from jax import lax
from jax.experimental import pallas as pl
from jax.experimental.pallas import tpu as pltpu
from jax.sharding import PartitionSpec as P

CZ, CY, CX = 32, 16, 128
ROWS = CZ * CY
ANG, DW, NBLK = 8, 256, 4
V = CY * CX
R = 8
GZ, GY, GX = 4, 4, 8
BRICKS = GY * GX
CELLS = float(CZ * CY * CX * GZ * BRICKS)
MESH = pl.DeviceIdType.MESH
F32, BF16 = jnp.float32, jnp.bfloat16
STEP = 0.5
SHRINK = 0.2
EPS = 1e-6
CHUNK = 128
NCHUNK = V // CHUNK

RAW = [math.exp(-k * k / 12.5) for k in range(-R, R + 1)]
TAPS = [r / sum(RAW) for r in RAW]


def dot(a, b, dims):
    return lax.dot_general(a, b, (dims, ((), ())), preferred_element_type=F32)


def split(v):
    hi = v.astype(BF16)
    lo = (v - hi.astype(F32)).astype(BF16)
    return hi, lo


def kernel(
    start_ref, meas_ref, tiles_ref, tb_ref, row_ref,
    x_out, dual_out,
    raw, mat, tmp, x0, w1, w2, res, qbuf, xa, zbuf, zmid, ybuf, ymid, tbv, obs, mis, acc,
    zs, zr, zs2, zr2, ys, yr, ys2, yr2, xs, xr,
    fzs, fzr, fys, fyr, fxs, fxr,
    stage, sl, snd1, rcv1, snd2, rcv2,
    hterm, back, dl, dlm, xlr, bdl, fac,
    red0, redz, red1, redx,
    bx, wx, bx2, wx2,
    load_sem, tile_sem, z_send, z_recv, yx_send, yx_recv, f_send, f_recv,
    a_send, a_recv, rz_send, rz_recv, rx_send, rx_recv, out_sem,
):
    gz, gy, gx = lax.axis_index("gz"), lax.axis_index("gy"), lax.axis_index("gx")
    me = gy * GX + gx
    scope = jax.named_scope

    barrier = pltpu.get_barrier_semaphore()

    def member(t):
        d = lax.rem(me + t, BRICKS)
        return d, (gz, d // GX, lax.rem(d, GX))

    @pl.loop(1, BRICKS)
    def _(t):
        pl.semaphore_signal(barrier, inc=1, device_id=member(t)[1], device_id_type=MESH)

    @pl.loop(1, GZ)
    def _(t):
        pl.semaphore_signal(
            barrier, inc=1, device_id=(lax.rem(gz + t, GZ), gy, gx), device_id_type=MESH
        )

    ld = [
        pltpu.make_async_copy(start_ref, x0, load_sem.at[0]),
        pltpu.make_async_copy(meas_ref, obs, load_sem.at[1]),
    ]
    for c in ld:
        c.start()

    def tile_copy(c):
        rows = pl.ds(pl.multiple_of(c * CHUNK, CHUNK), CHUNK)
        return pltpu.make_async_copy(tiles_ref.at[rows], raw.at[rows], tile_sem.at[c])

    @pl.loop(0, NCHUNK)
    def _(c):
        tile_copy(c).start()

    def there(dz, dy, dx):
        ok = True
        for d, at, n in ((dz, gz, GZ), (dy, gy, GY), (dx, gx, GX)):
            if d:
                near = at > 0 if d < 0 else at < n - 1
                ok = near if ok is True else jnp.logical_and(ok, near)
        return ok

    class Hub:
        def __init__(self, items):
            self.items = [
                (
                    there(*d),
                    there(*(-i for i in d)),
                    pltpu.make_async_remote_copy(
                        src, dst, ss, rs,
                        device_id=(gz + d[0], gy + d[1], gx + d[2]), device_id_type=MESH,
                    ),
                    dst,
                )
                for d, src, dst, ss, rs in items
            ]

        def clear(self):
            for _, arrives, _, dst in self.items:

                @pl.when(jnp.logical_not(arrives))
                def _():
                    dst[...] = jnp.zeros(dst.shape, dst.dtype)

        def start(self):
            for leaves, _, copy, _ in self.items:
                pl.when(leaves)(copy.start)

        def wait_recv(self):
            for _, arrives, copy, _ in self.items:
                pl.when(arrives)(copy.wait_recv)

        def wait_send(self):
            for leaves, _, copy, _ in self.items:
                pl.when(leaves)(copy.wait_send)

    def pair(axis, src, dst, send, recv):
        unit = [int(axis == a) for a in range(3)]
        return [
            ([-u for u in unit], src.at[0], dst.at[1], send.at[0], recv.at[0]),
            (unit, src.at[1], dst.at[0], send.at[1], recv.at[1]),
        ]

    def around(m, low, high, into_low, into_high):
        items = [
            ((0, -1, 0), low, into_high, yx_send.at[m, 0], yx_recv.at[m, 0]),
            ((0, 1, 0), high, into_low, yx_send.at[m, 1], yx_recv.at[m, 1]),
        ]
        k = 2
        for sy in (0, -1, 1):
            for side, sx in ((0, -1), (1, 1)):
                items.append((
                    (0, sy, sx), xs.at[m, side], xr.at[m, 1 - sy, 1 - side],
                    yx_send.at[m, k], yx_recv.at[m, k],
                ))
                k += 1
        return Hub(items)

    zhub = [Hub(pair(0, zs.at[n], zr.at[n], z_send.at[n], z_recv.at[n])) for n in range(3)]
    zhub2 = Hub(pair(0, zs2, zr2, z_send.at[3], z_recv.at[3]))
    yxhub = [around(n, ys.at[n, 0], ys.at[n, 1], yr.at[n, 0], yr.at[n, 1]) for n in range(4)]
    yxhub2 = around(4, ys2, ys2, yr2.at[0], yr2.at[1])
    fhub = [
        Hub(
            pair(0, fzs.at[n], fzr.at[n], f_send.at[n, 0], f_recv.at[n, 0])
            + pair(1, fys.at[n], fyr.at[n], f_send.at[n, 1], f_recv.at[n, 1])
            + pair(2, fxs.at[n], fxr.at[n], f_send.at[n, 2], f_recv.at[n, 2])
        )
        for n in range(3)
    ]
    hubs = zhub + [zhub2] + yxhub + [yxhub2] + fhub
    for h in hubs:
        h.clear()

    def gauss(d):
        df = d.astype(F32)
        w = jnp.exp(df * df * (-1.0 / 12.5)) * (1.0 / sum(RAW))
        return jnp.where(jnp.abs(d) <= R, w, 0.0)

    def iota(shape, axis):
        return lax.broadcasted_iota(jnp.int32, shape, axis)

    square = (CX, CX)
    bhi, blo = split(gauss(iota(square, 0) - iota(square, 1)))
    bx[0:CX] = bhi
    bx[CX : 2 * CX] = bhi
    bx[2 * CX : 3 * CX] = blo
    k0, k1 = iota((32, CX), 0), iota((32, CX), 1)
    pos = jnp.where(k0 < 16, lax.rem(k0, 8) - 8, CX + lax.rem(k0, 8))
    whi, wlo = split(gauss(pos - k1))
    wx[0:32] = whi
    wx[32:64] = wlo
    rim = ((k1 == 0) & ((k0 == 7) | (k0 == 15))) | ((k1 == CX - 1) & ((k0 == 16) | (k0 == 24)))
    wx[64:96] = jnp.where(rim, 1.0, 0.0).astype(BF16)
    s0, s1 = iota((32, 2 * CX), 0), iota((32, 2 * CX), 1)
    want = jnp.where(s0 < 16, lax.rem(s0, 8), CX - 8 + lax.rem(s0, 8)) + jnp.where(
        lax.rem(s0, 16) < 8, 0, CX
    )
    pick = jnp.where(s1 == want, 1.0, 0.0).astype(BF16)
    pick2 = jnp.where(k1 == jnp.where(k0 < 16, k0, CX - 32 + k0), 1.0, 0.0).astype(BF16)

    wide = (GX, GX * CX)
    spread = jnp.where(iota(wide, 0) == iota(wide, 1) // CX, 1.0, 0.0).astype(BF16)
    for b in range(GY):
        rows = dot(tb_ref[b].astype(F32).astype(BF16), spread, ((0,), (0,)))
        for c in range(GX):
            tbv[b * GX + c] = rows[:, c * CX : (c + 1) * CX]

    def relayout(low, high):
        @pl.loop(low, high)
        def _(c):
            tile_copy(c).wait()
            rows = pl.ds(pl.multiple_of(c * CHUNK, CHUNK), CHUNK)
            block = raw[rows].astype(F32).reshape(CHUNK * ANG, DW)
            for h in range(2):
                tmp[h] = block[:, h * 128 : (h + 1) * 128]
            for a in range(ANG):
                for h in range(2):
                    part = tmp[h, pl.ds(a, CHUNK, stride=ANG), :]
                    mat[rows, a * DW + h * 128 : a * DW + (h + 1) * 128] = part.astype(BF16)

    for c in ld:
        c.wait()
    for a in range(ANG):
        acc[pl.ds(a, 1), :] = obs[0, pl.ds(row_ref[a], 1), :]

    relayout(0, 6)
    with scope("wait_barrier"):
        pl.semaphore_wait(barrier, BRICKS - 1 + GZ - 1)

    def send_faces(n, src):
        fzs[n, 0] = src[0]
        fzs[n, 1] = src[CZ - 1]
        v = src[...]
        fys[n, 0] = v[:, 0, :]
        fys[n, 1] = v[:, CY - 1, :]
        hi, lo = split(v.reshape(ROWS, CX))
        f = dot(pick, jnp.concatenate([hi, lo], axis=1), ((1,), (1,))).astype(BF16)
        fxs[n, 0] = f[0:16]
        fxs[n, 1] = f[16:32]
        fhub[n].start()

    def send_z(n, src):
        zs[n, 0] = src[0:R].reshape(R * CY, CX).astype(BF16)
        zs[n, 1] = src[CZ - R : CZ].reshape(R * CY, CX).astype(BF16)
        zhub[n].start()

    def taps(at):
        t = TAPS[R] * at(R)
        for k in range(R):
            t += TAPS[k] * (at(k) + at(2 * R - k))
        return t

    def blur_z(n, src, out):
        zbuf[R : R + CZ] = src[...]
        with scope("wait_z"):
            zhub[n].wait_recv()
        zbuf[0:R] = zr[n, 0].astype(F32).reshape(R, CY, CX)
        zbuf[R + CZ : 2 * R + CZ] = zr[n, 1].astype(F32).reshape(R, CY, CX)

        @pl.loop(0, CZ, unroll=2)
        def _(z):
            out[z] = taps(lambda k: zbuf[z + k])

    def send_yx(n, w):
        v = w[...]
        ys[n, 0] = v[:, 0:R, :].reshape(CZ * R, CX).astype(BF16)
        ys[n, 1] = v[:, CY - R :, :].reshape(CZ * R, CX).astype(BF16)
        hi, lo = split(v.reshape(ROWS, CX))
        f = dot(pick, jnp.concatenate([hi, lo], axis=1), ((1,), (1,))).astype(BF16)
        xs[n, 0] = f[0:16]
        xs[n, 1] = f[16:32]
        yxhub[n].start()

    def rows_of(m, slot, weights):
        halo = xr[m, slot].reshape(32, ROWS)
        return dot(jnp.concatenate([halo, halo], axis=0), weights, ((0,), (0,)))

    def own_rows(w, mat3):
        hi, lo = split(w[...].reshape(ROWS, CX))
        both = jnp.concatenate([hi, lo], axis=1)
        return dot(both, mat3[0 : 2 * CX], ((1,), (0,))) + dot(hi, mat3[2 * CX :], ((1,), (0,)))

    def blur_yx(n, w, out):
        own = own_rows(w, bx)
        ybuf[:, R : R + CY, :] = own.reshape(CZ, CY, CX)
        with scope("wait_yx"):
            yxhub[n].wait_recv()
        ybuf[:, R : R + CY, :] += rows_of(n, 1, wx[0:64]).reshape(CZ, CY, CX)
        for side, at in ((0, slice(CY - R, CY)), (1, slice(0, R))):
            y = yr[n, side]
            rows = dot(jnp.concatenate([y, y], axis=1), bx[CX:], ((1,), (0,)))
            more = rows_of(n, 2 * side, wx[0:64]).reshape(CZ, CY, CX)[:, at, :]
            to = slice(0, R) if side == 0 else slice(R + CY, 2 * R + CY)
            ybuf[:, to, :] = rows.reshape(CZ, R, CX) + more

        @pl.loop(0, CZ, unroll=2)
        def _(z):
            out[z] = taps(lambda k: ybuf[z, k : k + CY, :])

    lane, sub = iota((CY, CX), 1), iota((CY, CX), 0)
    ends = ((gz == 0, gz == GZ - 1), (gy == 0, gy == GY - 1), (gx == 0, gx == GX - 1))

    def wait_faces(n):
        with scope("wait_faces"):
            fhub[n].wait_recv()
        xlr[...] = dot(fxr[n].reshape(32, ROWS), wx[64:96], ((0,), (0,))).reshape(CZ, CY, CX)
        xa[0] = fzr[n, 0]
        xa[CZ + 1] = fzr[n, 1]

    def diffs(n, z):
        v = xa[z + 1]
        up, low = xa[z + 2], xa[z]
        yield (
            jnp.where((z == CZ - 1) & ends[0][1], 0.0, up - v),
            jnp.where((z == 0) & ends[0][0], 0.0, v - low),
        )
        up = jnp.where(sub == CY - 1, fyr[n, 1, pl.ds(z, 1), :], pltpu.roll(v, CY - 1, 0))
        low = jnp.where(sub == 0, fyr[n, 0, pl.ds(z, 1), :], pltpu.roll(v, 1, 0))
        yield (
            jnp.where((sub == CY - 1) & ends[1][1], 0.0, up - v),
            jnp.where((sub == 0) & ends[1][0], 0.0, v - low),
        )
        edge = xlr[z]
        up = jnp.where(lane == CX - 1, edge, pltpu.roll(v, CX - 1, 1))
        low = jnp.where(lane == 0, edge, pltpu.roll(v, 1, 1))
        yield (
            jnp.where((lane == CX - 1) & ends[2][1], 0.0, up - v),
            jnp.where((lane == 0) & ends[2][0], 0.0, v - low),
        )

    def fold(p):
        return p[0:8] + p[8:16]

    def redz_copy(n, t):
        return pltpu.make_async_remote_copy(
            red0.at[n], redz.at[n, t], rz_send.at[n, t], rz_recv.at[n, t],
            device_id=(lax.rem(gz + t, GZ), gy, gx), device_id_type=MESH,
        )

    def redx_copy(n, t):
        return pltpu.make_async_remote_copy(
            red1.at[n], redx.at[n, t], rx_send.at[n], rx_recv.at[n],
            device_id=member(t)[1], device_id_type=MESH,
        )

    def send_sums(n, primal, dualres):
        p = jnp.sum(jnp.sum(primal, axis=0, keepdims=True), axis=1, keepdims=True)
        d = jnp.sum(jnp.sum(dualres, axis=0, keepdims=True), axis=1, keepdims=True)
        red0[n] = jnp.where(lane[0:1] < CX // 2, p, d)
        for t in range(1, GZ):
            redz_copy(n, t).start()

    def forward_sums(n):
        total = red0[n]
        for t in range(1, GZ):
            redz_copy(n, t).wait_recv()
            total += redz[n, t]
        red1[n] = total

        @pl.loop(1, BRICKS)
        def _(t):
            redx_copy(n, t).start()

    def factor_of(n, penalty):
        total = red1[n]
        got = redx.at[n, pl.ds(1, BRICKS - 1)]
        pltpu.make_async_copy(got, got, rx_recv.at[n]).wait()
        total += jnp.sum(redx[n, 1:BRICKS], axis=0)
        p = jnp.broadcast_to(total[:, 0:1], (8, CX)) * (1.0 / (3.0 * CELLS))
        d = jnp.broadcast_to(total[:, CX - 1 : CX], (8, CX)) * (1.0 / CELLS)
        d = penalty * penalty * d
        return jnp.sqrt(jnp.sqrt((p + EPS) / (d + EPS)))

    def arrivals(ref, sem):
        got = ref.at[pl.ds(0, BRICKS - 1)]
        pltpu.make_async_copy(got, got, sem).wait()

    def send_block(n, i, src, dst, d, dev):
        pltpu.make_async_remote_copy(
            src.at[n, d], dst.at[n, me], a_send.at[n, i], a_recv.at[n, i],
            device_id=dev, device_id_type=MESH,
        ).start()

    def project(n):
        for z0 in range(1):
            for y in range(CY):
                sl[:, y * CX : (y + 1) * CX] = res[pl.ds(y, CZ, stride=CY), :].astype(BF16)
        with scope("mm_fwd"):
            for a in range(ANG):
                c = dot(sl[...], mat[:, a * DW : (a + 1) * DW], ((1,), (0,)))
                for h in range(2):
                    stage[h, pl.ds(a, CZ, stride=ANG), :] = c[:, h * 128 : (h + 1) * 128]

        def block_of(d):
            rows = pl.ds(pl.multiple_of(d * ANG, ANG), ANG)
            return jnp.concatenate([stage[0, rows, :], stage[1, rows, :]], axis=1).astype(BF16)

        @pl.loop(1, BRICKS)
        def _(t):
            d, dev = member(t)
            snd1[n, d] = block_of(d)
            send_block(n, 0, snd1, rcv1, d, dev)

        rcv1[n, me] = block_of(me)

    def return_misfit(n):
        with scope("wait_a1"):
            arrivals(rcv1.at[n], a_recv.at[n, 0])

        def add(s, sums):
            x = rcv1[n, s].astype(F32)
            t = tbv[s]
            t = jnp.concatenate([t, t], axis=1)
            return tuple(sums[q] + jnp.where(t == float(q), x, 0.0) for q in range(NBLK))

        sums = lax.fori_loop(
            0, BRICKS, add, tuple(jnp.zeros((ANG, DW), F32) for _ in range(NBLK)), unroll=2
        )
        for q in range(NBLK):
            cols = slice(q * DW, (q + 1) * DW)
            mis[:, cols] = (sums[q] - acc[:, cols]).astype(BF16).astype(F32)

        def chosen(d):
            t = tbv[d]
            t = jnp.concatenate([t, t], axis=1)
            c = mis[:, 0:DW]
            for q in range(1, NBLK):
                c = jnp.where(t == float(q), mis[:, q * DW : (q + 1) * DW], c)
            return c.astype(BF16)

        @pl.loop(1, BRICKS)
        def _(t):
            d, dev = member(t)
            snd2[n, d] = chosen(d)
            send_block(n, 1, snd2, rcv2, d, dev)

        rcv2[n, me] = chosen(me)

    def backproject(n, out):
        with scope("wait_a2"):
            arrivals(rcv2.at[n], a_recv.at[n, 1])
        r = rcv2[n].astype(F32).reshape(CZ * ANG, DW)
        for h in range(2):
            stage[h] = r[:, h * 128 : (h + 1) * 128]
        for a in range(ANG):
            for h in range(2):
                sl[:, a * DW + h * 128 : a * DW + (h + 1) * 128] = stage[
                    h, pl.ds(a, CZ, stride=ANG), :
                ].astype(BF16)
        with scope("mm_bwd"):
            for c in range(ANG):
                b = dot(sl[...], mat[c * DW : (c + 1) * DW, :], ((1,), (1,)))
                for h in range(2):
                    res[pl.ds(2 * c + h, CZ, stride=CY), :] = b[:, h * 128 : (h + 1) * 128]
        out[...] = res[...].reshape(CZ, CY, CX)

    send_z(0, x0)
    send_faces(0, x0)
    relayout(6, 12)
    blur_z(0, x0, w1)
    send_yx(0, w1)
    relayout(12, NCHUNK)
    blur_yx(0, w1, w2)
    res[...] = w2[...].reshape(ROWS, CX)
    project(0)

    wait_faces(0)
    xa[1 : CZ + 1] = x0[...]
    cut = SHRINK

    @pl.loop(0, CZ, unroll=2)
    def _(z):
        smooth = jnp.zeros((CY, CX), F32)
        shrunk = jnp.zeros((CY, CX), F32)
        for j, jm in diffs(0, z):
            s = j - jnp.clip(j, -cut, cut)
            sm = jm - jnp.clip(jm, -cut, cut)
            smooth += jm - j
            shrunk += sm - s
        h = STEP * (smooth - shrunk)
        x0[z] = xa[z + 1] - h
        back[z] = shrunk

    send_z(1, x0)

    shape1, shape2 = (160, 256), (256, CX)
    i, m = iota(shape1, 0), iota(shape1, 1) - 8
    i = jnp.where(i < CX, i, jnp.where(i < CX + 16, i - CX - 16, i - 16))
    inside = ((m >= 0) | (gx > 0)) & ((m < CX) | (gx < GX - 1)) & (m < CX + 8)
    thi, tlo = split(jnp.where(inside, gauss(i - m), 0.0))
    m = iota(shape2, 0) - 8
    uhi, ulo = split(gauss(m - iota(shape2, 1)))
    twice = (
        dot(thi, uhi, ((1,), (0,))) + dot(thi, ulo, ((1,), (0,))) + dot(tlo, uhi, ((1,), (0,)))
    )
    bhi, blo = split(twice[0:CX])
    bx2[0:CX] = bhi
    bx2[CX : 2 * CX] = bhi
    bx2[2 * CX : 3 * CX] = blo
    whi, wlo = split(twice[CX : CX + 32])
    wx2[0:32] = whi
    wx2[32:64] = wlo

    return_misfit(0)
    blur_z(1, x0, w1)
    send_yx(1, w1)
    backproject(0, w2)

    zs2[0] = w2[0:16].reshape(16 * CY, CX).astype(BF16)
    zs2[1] = w2[CZ - 16 : CZ].reshape(16 * CY, CX).astype(BF16)
    zhub2.start()
    blur_yx(1, w1, qbuf)
    zbuf[16 : 16 + CZ] = w2[...]
    with scope("wait_z2"):
        zhub2.wait_recv()
    zbuf[0:16] = zr2[0].astype(F32).reshape(16, CY, CX)
    zbuf[16 + CZ : 32 + CZ] = zr2[1].astype(F32).reshape(16, CY, CX)

    @pl.loop(0, CZ + 16, unroll=2)
    def _(z):
        out = ((z < 8) & ends[0][0]) | ((z >= CZ + 8) & ends[0][1])
        zmid[z] = jnp.where(out, 0.0, taps(lambda k: zbuf[z + k]))

    @pl.loop(0, CZ, unroll=2)
    def _(z):
        w2[z] = taps(lambda k: zmid[z + k])

    hi = w2[...].reshape(ROWS, CX).astype(BF16)
    ys2[...] = hi
    f = dot(pick2, hi, ((1,), (1,))).astype(BF16)
    xs[4, 0] = f[0:16]
    xs[4, 1] = f[16:32]
    yxhub2.start()
    w1[...] = zmid[8 : 8 + CZ]
    send_yx(2, w1)

    ymid[:, 16 : 16 + CY, :] = own_rows(w2, bx2).reshape(CZ, CY, CX)
    with scope("wait_yx2"):
        yxhub2.wait_recv()
    ymid[:, 16 : 16 + CY, :] += rows_of(4, 1, wx2[...]).reshape(CZ, CY, CX)
    for side in range(2):
        y = yr2[side]
        rows = dot(jnp.concatenate([y, y], axis=1), bx2[CX:], ((1,), (0,)))
        rows = rows + rows_of(4, 2 * side, wx2[...])
        ymid[:, 32 * side : 32 * side + 16, :] = rows.reshape(CZ, CY, CX)
    sub2 = iota((CY + 16, CX), 0)
    outside = ((sub2 < 8) & ends[1][0]) | ((sub2 >= CY + 8) & ends[1][1])

    @pl.loop(0, CZ, unroll=2)
    def _(z):
        ybuf[z] = jnp.where(outside, 0.0, taps(lambda k: ymid[z, k : k + CY + 16, :]))

    @pl.loop(0, CZ, unroll=2)
    def _(z):
        rows = pl.ds(pl.multiple_of(z * CY, CY), CY)
        res[rows, :] = qbuf[z] - STEP * taps(lambda k: ybuf[z, k : k + CY, :])

    project(1)
    blur_yx(2, w1, w2)
    x0[...] = x0[...] - STEP * w2[...]
    send_faces(1, x0)
    xa[1 : CZ + 1] = x0[...]
    return_misfit(1)
    wait_faces(1)

    def one(z, sums):
        primal, dres = sums
        smooth = jnp.zeros((CY, CX), F32)
        shrunk = jnp.zeros((CY, CX), F32)
        bdual = jnp.zeros((CY, CX), F32)
        for axis, (j, jm) in enumerate(diffs(1, z)):
            s = j - jnp.clip(j, -cut, cut)
            sm = jm - jnp.clip(jm, -cut, cut)
            d = j - s
            dm = jm - sm
            smooth += jm - j
            shrunk += sm - s
            bdual += dm - d
            dl[axis, z] = d
            dlm[axis, z] = dm
            primal += fold(jnp.square(j - s))
        dres += fold(jnp.square(shrunk - back[z]))
        hterm[z] = smooth - shrunk
        back[z] = shrunk
        bdl[z] = bdual
        return primal, dres

    zero = jnp.zeros((8, CX), F32)
    primal, dres = lax.fori_loop(0, CZ, one, (zero, zero), unroll=2)
    send_sums(0, primal, dres)
    backproject(1, w2)
    send_z(2, w2)
    forward_sums(0)
    blur_z(2, w2, w1)
    send_yx(3, w1)
    penalty = factor_of(0, jnp.ones((8, CX), F32))
    inv1 = 1.0 / penalty
    pen3 = penalty[0:1].reshape(1, 1, CX)
    inv3 = inv1[0:1].reshape(1, 1, CX)
    x0[...] = x0[...] - STEP * pen3 * (hterm[...] + bdl[...] * inv3)
    blur_yx(3, w1, w2)
    x0[...] = x0[...] - STEP * w2[...]
    send_faces(2, x0)
    x_copy = pltpu.make_async_copy(x0, x_out, out_sem.at[0])
    x_copy.start()
    xa[1 : CZ + 1] = x0[...]
    wait_faces(2)
    cut2 = (SHRINK / penalty)[0:1]
    inv = inv1[0:1]

    def last(z, sums):
        primal, dres = sums
        shrunk = jnp.zeros((CY, CX), F32)
        for axis, (j, jm) in enumerate(diffs(2, z)):
            t = j + dl[axis, z] * inv
            tm = jm + dlm[axis, z] * inv
            s = t - jnp.clip(t, -cut2, cut2)
            sm = tm - jnp.clip(tm, -cut2, cut2)
            shrunk += sm - s
            dl[axis, z] = t - s
            primal += fold(jnp.square(j - s))
        dres += fold(jnp.square(shrunk - back[z]))
        return primal, dres

    with scope("last"):
        primal, dres = lax.fori_loop(0, CZ, last, (zero, zero), unroll=2)
    send_sums(1, primal, dres)
    with scope("sums_z"):
        forward_sums(1)
    with scope("sums_x"):
        factor2 = factor_of(1, penalty)
    scale = (1.0 / factor2)[0:1].reshape(1, 1, 1, CX)
    dl[...] = dl[...] * scale
    d_copy = pltpu.make_async_copy(dl, dual_out, out_sem.at[1])
    d_copy.start()

    with scope("wait_sends"):
        for h in hubs:
            h.wait_send()
        for n in range(2):
            for i, ref in enumerate((snd1, snd2)):
                arrivals(ref.at[n], a_send.at[n, i])
            for t in range(1, GZ):
                redz_copy(n, t).wait_send()
            got = redx.at[n, pl.ds(1, BRICKS - 1)]
            pltpu.make_async_copy(got, got, rx_send.at[n]).wait()
    x_copy.wait()
    d_copy.wait()


def body(start, measured, tiles, tile_block, angle_row):
    vm = pltpu.VMEM
    dma = pltpu.SemaphoreType.DMA
    block = vm((CZ, CY, CX), F32)
    return pl.pallas_call(
        kernel,
        out_shape=(
            jax.ShapeDtypeStruct((CZ, CY, CX), F32),
            jax.ShapeDtypeStruct((3, CZ, CY, CX), F32),
        ),
        in_specs=[
            pl.BlockSpec(memory_space=pl.ANY),
            pl.BlockSpec(memory_space=pl.ANY),
            pl.BlockSpec(memory_space=pl.ANY),
            pl.BlockSpec(memory_space=pltpu.VMEM),
            pl.BlockSpec(memory_space=pltpu.SMEM),
        ],
        out_specs=(pl.BlockSpec(memory_space=pl.ANY), pl.BlockSpec(memory_space=pl.ANY)),
        scratch_shapes=[
            vm((V, ANG, DW), BF16),
            vm((V, ANG * DW), BF16),
            vm((2, CHUNK * ANG, 128), F32),
            block, block, block,
            vm((ROWS, CX), F32),
            block,
            vm((CZ + 2, CY, CX), F32),
            vm((CZ + 32, CY, CX), F32),
            vm((CZ + 16, CY, CX), F32),
            vm((CZ, CY + 16, CX), F32),
            vm((CZ, CY + 32, CX), F32),
            vm((BRICKS, ANG, CX), F32),
            vm((1, ANG, NBLK * DW), F32),
            vm((ANG, NBLK * DW), F32),
            vm((ANG, NBLK * DW), F32),
            vm((3, 2, R * CY, CX), BF16),
            vm((3, 2, R * CY, CX), BF16),
            vm((2, 16 * CY, CX), BF16),
            vm((2, 16 * CY, CX), BF16),
            vm((4, 2, CZ * R, CX), BF16),
            vm((4, 2, CZ * R, CX), BF16),
            vm((ROWS, CX), BF16),
            vm((2, ROWS, CX), BF16),
            vm((5, 2, 16, ROWS), BF16),
            vm((5, 3, 2, 16, ROWS), BF16),
            vm((3, 2, CY, CX), F32),
            vm((3, 2, CY, CX), F32),
            vm((3, 2, CZ, CX), F32),
            vm((3, 2, CZ, CX), F32),
            vm((3, 2, 16, ROWS), BF16),
            vm((3, 2, 16, ROWS), BF16),
            vm((2, CZ * ANG, 128), F32),
            vm((CZ, V), BF16),
            vm((2, BRICKS, ANG, DW), BF16),
            vm((2, BRICKS, ANG, DW), BF16),
            vm((2, BRICKS, ANG, DW), BF16),
            vm((2, BRICKS, ANG, DW), BF16),
            block, block,
            vm((3, CZ, CY, CX), F32),
            vm((3, CZ, CY, CX), F32),
            block, block,
            vm((8, CX), F32),
            vm((2, 1, CX), F32),
            vm((2, GZ, 1, CX), F32),
            vm((2, 1, CX), F32),
            vm((2, BRICKS, 1, CX), F32),
            vm((3 * CX, CX), BF16),
            vm((96, CX), BF16),
            vm((3 * CX, CX), BF16),
            vm((64, CX), BF16),
            dma((2,)),
            dma((NCHUNK,)),
            dma((4, 2)),
            dma((4, 2)),
            dma((5, 8)),
            dma((5, 8)),
            dma((3, 3, 2)),
            dma((3, 3, 2)),
            dma((2, 2)),
            dma((2, 2)),
            dma((2, GZ)),
            dma((2, GZ)),
            dma((2,)),
            dma((2,)),
            dma((2,)),
        ],
        compiler_params=pltpu.CompilerParams(
            collective_id=0, has_side_effects=True, vmem_limit_bytes=60 * 1024 * 1024
        ),
    )(start, measured, tiles, tile_block, angle_row)


def solution(mesh):
    return jax.shard_map(
        body,
        mesh=mesh,
        in_specs=(
            P("gz", "gy", "gx"),
            P(("gz", "gy", "gx"), None, None),
            P("gy", None, "gx"),
            P(),
            P(),
        ),
        out_specs=(P("gz", "gy", "gx"), P(None, "gz", "gy", "gx")),
        check_vma=False,
    )
```

time: 104 us -> 88.8 us (0.85)
  Pallas kernels: 99.1 us -> 84.2 us
    pallas_call x1, Pallas kernels: 99.1 us -> 84.2 us  [body(): pl.pallas_call(kernel, out_shape=(jax.ShapeDtypeStruct((CZ, CY, CX), F32)...]
where the time goes in v2:
time: 88.8 us; the launch traced here: 88.6 us
  Pallas kernels  84.2 us (95%)
  local copies, waits for them, and re-layouts  3.73 us (4%)
    pallas_call x1, Pallas kernels, body(): pl.pallas_call(kernel, out_shape=(jax.ShapeDtypeStruct((CZ, CY, CX), F32)...  84.2 us
    unnamed x2, local copies, waits for them, and re-layouts  3.73 us

profile of v2, /device:TPU:1, one launch (start us, length us, event | category | flops | bytes accessed | tf_op | source)
XLA Modules:
  0.0 88.6 jit_solution(16338069236565485632)
XLA Ops:
  0.6 84.2 %shard_map.68 = (f32[32,16,128]{2,1,0:T(8,128)}, f32[3,32,16,128]{3,2,1,0:T(8,128)}) custom-call(f32[32,16,128]{2,1,0:T(8,128)} %start_ref.1, f32[1,8,1024]{2,1,0:T(8,128)} %meas_ref.1, bf16[2048,8,256]{2,1,0:T(8,128)(2,1)} %tiles_ref.1, s32[4,8,8]{2,1,0:T(8,128)} %tb_ref.1, s32[8]{0:T(128)} %row_ref.1), custom_call_target="tpu_custom_call" | custom-call | tf_op jit(solution)/shard_map/pallas_call | solution.py:649
  84.8 1.7 %copy.9 = f32[32,16,128]{2,1,0:T(8,128)} copy(f32[32,16,128]{2,1,0:T(8,128)} %get-tuple-element.4) | data formatting | bytes 524288
  86.5 2.1 %copy.10 = f32[3,32,16,128]{3,2,1,0:T(8,128)} copy(f32[3,32,16,128]{3,2,1,0:T(8,128)} %get-tuple-element.5) | data formatting | bytes 1572864

commit v3 on v2

--- a/solution.py
+++ b/solution.py
@@ -22,6 +22,11 @@
 EPS = 1e-6
 CHUNK = 128
 NCHUNK = V // CHUNK
+ORDER = sorted(
+    ((dx, dz, dc) for dz in range(4) for dx in range(4) for dc in range(2) if dx or dz or dc),
+    key=lambda s: -(min(s[0], 4 - s[0]) + min(s[1], 4 - s[1])),
+)
+SPLIT = 5
 
 RAW = [math.exp(-k * k / 12.5) for k in range(-R, R + 1)]
 TAPS = [r / sum(RAW) for r in RAW]
@@ -44,11 +49,11 @@
     zs, zr, zs2, zr2, ys, yr, ys2, yr2, xs, xr,
     fzs, fzr, fys, fyr, fxs, fxr,
     stage, sl, snd1, rcv1, snd2, rcv2,
-    hterm, back, dl, dlm, xlr, bdl, fac,
+    hterm, back, dl, dlm, xlr, bdl,
     red0, redz, red1, redx,
     bx, wx, bx2, wx2,
     load_sem, tile_sem, z_send, z_recv, yx_send, yx_recv, f_send, f_recv,
-    a_send, a_recv, rz_send, rz_recv, rx_send, rx_recv, out_sem,
+    a_send, a_recv, rz_send, rz_recv, rx_send, rx_recv,
 ):
     gz, gy, gx = lax.axis_index("gz"), lax.axis_index("gy"), lax.axis_index("gx")
     me = gy * GX + gx
@@ -56,12 +61,18 @@
 
     barrier = pltpu.get_barrier_semaphore()
 
+    chip_x = 2 * (gy // 2) + lax.rem(gx, 2)
+    chip_z, core = gx // 2, lax.rem(gy, 2)
+
     def member(t):
-        d = lax.rem(me + t, BRICKS)
-        return d, (gz, d // GX, lax.rem(d, GX))
-
-    @pl.loop(1, BRICKS)
-    def _(t):
+        dx, dz, dc = ORDER[t - 1]
+        x = lax.rem(chip_x + dx, 4)
+        z = lax.rem(chip_z + dz, 4)
+        y = 2 * (x // 2) + lax.rem(core + dc, 2)
+        x = 2 * z + lax.rem(x, 2)
+        return y * GX + x, (gz, y, x)
+
+    for t in range(1, BRICKS):
         pl.semaphore_signal(barrier, inc=1, device_id=member(t)[1], device_id_type=MESH)
 
     @pl.loop(1, GZ)
@@ -217,7 +228,6 @@
     for a in range(ANG):
         acc[pl.ds(a, 1), :] = obs[0, pl.ds(row_ref[a], 1), :]
 
-    relayout(0, 6)
     with scope("wait_barrier"):
         pl.semaphore_wait(barrier, BRICKS - 1 + GZ - 1)
 
@@ -351,8 +361,7 @@
             total += redz[n, t]
         red1[n] = total
 
-        @pl.loop(1, BRICKS)
-        def _(t):
+        for t in range(1, BRICKS):
             redx_copy(n, t).start()
 
     def factor_of(n, penalty):
@@ -389,8 +398,7 @@
             rows = pl.ds(pl.multiple_of(d * ANG, ANG), ANG)
             return jnp.concatenate([stage[0, rows, :], stage[1, rows, :]], axis=1).astype(BF16)
 
-        @pl.loop(1, BRICKS)
-        def _(t):
+        for t in range(1, BRICKS):
             d, dev = member(t)
             snd1[n, d] = block_of(d)
             send_block(n, 0, snd1, rcv1, d, dev)
@@ -422,8 +430,7 @@
                 c = jnp.where(t == float(q), mis[:, q * DW : (q + 1) * DW], c)
             return c.astype(BF16)
 
-        @pl.loop(1, BRICKS)
-        def _(t):
+        for t in range(1, BRICKS):
             d, dev = member(t)
             snd2[n, d] = chosen(d)
             send_block(n, 1, snd2, rcv2, d, dev)
@@ -450,10 +457,10 @@
 
     send_z(0, x0)
     send_faces(0, x0)
-    relayout(6, 12)
+    relayout(0, SPLIT)
     blur_z(0, x0, w1)
     send_yx(0, w1)
-    relayout(12, NCHUNK)
+    relayout(SPLIT, NCHUNK)
     blur_yx(0, w1, w2)
     res[...] = w2[...].reshape(ROWS, CX)
     project(0)
@@ -526,11 +533,11 @@
     xs[4, 1] = f[16:32]
     yxhub2.start()
     w1[...] = zmid[8 : 8 + CZ]
-    send_yx(2, w1)
 
     ymid[:, 16 : 16 + CY, :] = own_rows(w2, bx2).reshape(CZ, CY, CX)
     with scope("wait_yx2"):
         yxhub2.wait_recv()
+    send_yx(2, w1)
     ymid[:, 16 : 16 + CY, :] += rows_of(4, 1, wx2[...]).reshape(CZ, CY, CX)
     for side in range(2):
         y = yr2[side]
@@ -595,8 +602,7 @@
     blur_yx(3, w1, w2)
     x0[...] = x0[...] - STEP * w2[...]
     send_faces(2, x0)
-    x_copy = pltpu.make_async_copy(x0, x_out, out_sem.at[0])
-    x_copy.start()
+    x_out[...] = x0[...]
     xa[1 : CZ + 1] = x0[...]
     wait_faces(2)
     cut2 = (SHRINK / penalty)[0:1]
@@ -624,9 +630,7 @@
     with scope("sums_x"):
         factor2 = factor_of(1, penalty)
     scale = (1.0 / factor2)[0:1].reshape(1, 1, 1, CX)
-    dl[...] = dl[...] * scale
-    d_copy = pltpu.make_async_copy(dl, dual_out, out_sem.at[1])
-    d_copy.start()
+    dual_out[...] = dl[...] * scale
 
     with scope("wait_sends"):
         for h in hubs:
@@ -638,8 +642,6 @@
                 redz_copy(n, t).wait_send()
             got = redx.at[n, pl.ds(1, BRICKS - 1)]
             pltpu.make_async_copy(got, got, rx_send.at[n]).wait()
-    x_copy.wait()
-    d_copy.wait()
 
 
 def body(start, measured, tiles, tile_block, angle_row):
@@ -649,17 +651,17 @@
     return pl.pallas_call(
         kernel,
         out_shape=(
-            jax.ShapeDtypeStruct((CZ, CY, CX), F32),
-            jax.ShapeDtypeStruct((3, CZ, CY, CX), F32),
+            pltpu.VMEM((CZ, CY, CX), F32),
+            pltpu.VMEM((3, CZ, CY, CX), F32),
         ),
         in_specs=[
-            pl.BlockSpec(memory_space=pl.ANY),
-            pl.BlockSpec(memory_space=pl.ANY),
-            pl.BlockSpec(memory_space=pl.ANY),
+            pl.BlockSpec(memory_space=pltpu.HBM),
+            pl.BlockSpec(memory_space=pltpu.HBM),
+            pl.BlockSpec(memory_space=pltpu.HBM),
             pl.BlockSpec(memory_space=pltpu.VMEM),
             pl.BlockSpec(memory_space=pltpu.SMEM),
         ],
-        out_specs=(pl.BlockSpec(memory_space=pl.ANY), pl.BlockSpec(memory_space=pl.ANY)),
+        out_specs=(pl.BlockSpec(memory_space=pltpu.VMEM), pl.BlockSpec(memory_space=pltpu.VMEM)),
         scratch_shapes=[
             vm((V, ANG, DW), BF16),
             vm((V, ANG * DW), BF16),
@@ -702,7 +704,6 @@
             vm((3, CZ, CY, CX), F32),
             vm((3, CZ, CY, CX), F32),
             block, block,
-            vm((8, CX), F32),
             vm((2, 1, CX), F32),
             vm((2, GZ, 1, CX), F32),
             vm((2, 1, CX), F32),
@@ -725,7 +726,6 @@
             dma((2, GZ)),
             dma((2,)),
             dma((2,)),
-            dma((2,)),
         ],
         compiler_params=pltpu.CompilerParams(
             collective_id=0, has_side_effects=True, vmem_limit_bytes=60 * 1024 * 1024

time: 88.8 us -> 83.1 us (0.936)
  Pallas kernels: 84.2 us -> 80.8 us
  local copies, waits for them, and re-layouts: 3.73 us -> 1.58 us
    pallas_call x1, Pallas kernels: 84.2 us -> 80.8 us  [body(): pl.pallas_call(kernel, out_shape=(pltpu.VMEM((CZ, CY, CX), F32), pltpu.VM...]
    unnamed x2, local copies, waits for them, and re-layouts: 3.73 us -> 1.58 us
where the time goes in v3:
time: 83.1 us; the launch traced here: 83 us
  Pallas kernels  80.8 us (97%)
  local copies, waits for them, and re-layouts  1.58 us (2%)
    pallas_call x1, Pallas kernels, body(): pl.pallas_call(kernel, out_shape=(pltpu.VMEM((CZ, CY, CX), F32), pltpu.VM...  80.8 us

profile of v3, /device:TPU:1, one launch (start us, length us, event | category | flops | bytes accessed | tf_op | source)
XLA Modules:
  0.0 83.0 jit_solution(9468971242912367935)
XLA Ops:
  0.6 80.8 %shard_map.68 = (f32[32,16,128]{2,1,0:T(8,128)S(1)}, f32[3,32,16,128]{3,2,1,0:T(8,128)S(1)}) custom-call(f32[32,16,128]{2,1,0:T(8,128)} %start_ref.1, f32[1,8,1024]{2,1,0:T(8,128)} %meas_ref.1, bf16[2048,8,256]{2,1,0:T(8,128)(2,1)} %tiles_ref.1, s32[4,8,8]{2,1,0:T(8,128)} %tb_ref.1, s32[8]{0:T(128)} %row_ref.1), custom_call_target="tpu_custom_call" | custom-call | tf_op jit(solution)/shard_map/pallas_call | solution.py:651
  81.4 0.7 copy.9
  82.1 0.9 %copy.10 = f32[3,32,16,128]{3,2,1,0:T(8,128)} copy(f32[3,32,16,128]{3,2,1,0:T(8,128)S(1)} %get-tuple-element.3) | data formatting | bytes 1572864

commit v4 on v3

--- a/solution.py
+++ b/solution.py
@@ -27,6 +27,13 @@
     key=lambda s: -(min(s[0], 4 - s[0]) + min(s[1], 4 - s[1])),
 )
 SPLIT = 5
+ORDER_ALL = sorted(
+    ((dy, t) for dy in range(GZ) for t in range(GY * GX) if dy or t),
+    key=lambda s: -(
+        min(s[0], 4 - s[0])
+        + (sum(min(d, 4 - d) for d in ORDER[s[1] - 1][:2]) if s[1] else 0)
+    ),
+)
 
 RAW = [math.exp(-k * k / 12.5) for k in range(-R, R + 1)]
 TAPS = [r / sum(RAW) for r in RAW]
@@ -50,10 +57,10 @@
     fzs, fzr, fys, fyr, fxs, fxr,
     stage, sl, snd1, rcv1, snd2, rcv2,
     hterm, back, dl, dlm, xlr, bdl,
-    red0, redz, red1, redx,
+    red0, redz, red1, redx, redall,
     bx, wx, bx2, wx2,
     load_sem, tile_sem, z_send, z_recv, yx_send, yx_recv, f_send, f_recv,
-    a_send, a_recv, rz_send, rz_recv, rx_send, rx_recv,
+    a_send, a_recv, rz_send, rz_recv, rx_send, rx_recv, all_send, all_recv,
 ):
     gz, gy, gx = lax.axis_index("gz"), lax.axis_index("gy"), lax.axis_index("gx")
     me = gy * GX + gx
@@ -347,12 +354,18 @@
             device_id=member(t)[1], device_id_type=MESH,
         )
 
-    def send_sums(n, primal, dualres):
+    def put_sums(n, primal, dualres):
         p = jnp.sum(jnp.sum(primal, axis=0, keepdims=True), axis=1, keepdims=True)
         d = jnp.sum(jnp.sum(dualres, axis=0, keepdims=True), axis=1, keepdims=True)
         red0[n] = jnp.where(lane[0:1] < CX // 2, p, d)
-        for t in range(1, GZ):
-            redz_copy(n, t).start()
+
+    def send_all():
+        for slot, (dy, t) in enumerate(ORDER_ALL):
+            dev = (gy, gx) if t == 0 else member(t)[1][1:]
+            pltpu.make_async_remote_copy(
+                red0.at[1], redall.at[slot + 1], all_send, all_recv,
+                device_id=(lax.rem(gz + dy, GZ), *dev), device_id_type=MESH,
+            ).start()
 
     def forward_sums(n):
         total = red0[n]
@@ -369,6 +382,9 @@
         got = redx.at[n, pl.ds(1, BRICKS - 1)]
         pltpu.make_async_copy(got, got, rx_recv.at[n]).wait()
         total += jnp.sum(redx[n, 1:BRICKS], axis=0)
+        return factor_from(total, penalty)
+
+    def factor_from(total, penalty):
         p = jnp.broadcast_to(total[:, 0:1], (8, CX)) * (1.0 / (3.0 * CELLS))
         d = jnp.broadcast_to(total[:, CX - 1 : CX], (8, CX)) * (1.0 / CELLS)
         d = penalty * penalty * d
@@ -588,7 +604,9 @@
 
     zero = jnp.zeros((8, CX), F32)
     primal, dres = lax.fori_loop(0, CZ, one, (zero, zero), unroll=2)
-    send_sums(0, primal, dres)
+    put_sums(0, primal, dres)
+    for t in range(1, GZ):
+        redz_copy(0, t).start()
     backproject(1, w2)
     send_z(2, w2)
     forward_sums(0)
@@ -599,6 +617,8 @@
     pen3 = penalty[0:1].reshape(1, 1, CX)
     inv3 = inv1[0:1].reshape(1, 1, CX)
     x0[...] = x0[...] - STEP * pen3 * (hterm[...] + bdl[...] * inv3)
+    dl[...] = dl[...] * inv3
+    dlm[...] = dlm[...] * inv3
     blur_yx(3, w1, w2)
     x0[...] = x0[...] - STEP * w2[...]
     send_faces(2, x0)
@@ -606,14 +626,13 @@
     xa[1 : CZ + 1] = x0[...]
     wait_faces(2)
     cut2 = (SHRINK / penalty)[0:1]
-    inv = inv1[0:1]
 
     def last(z, sums):
         primal, dres = sums
         shrunk = jnp.zeros((CY, CX), F32)
         for axis, (j, jm) in enumerate(diffs(2, z)):
-            t = j + dl[axis, z] * inv
-            tm = jm + dlm[axis, z] * inv
+            t = j + dl[axis, z]
+            tm = jm + dlm[axis, z]
             s = t - jnp.clip(t, -cut2, cut2)
             sm = tm - jnp.clip(tm, -cut2, cut2)
             shrunk += sm - s
@@ -623,14 +642,16 @@
         return primal, dres
 
     with scope("last"):
-        primal, dres = lax.fori_loop(0, CZ, last, (zero, zero), unroll=2)
-    send_sums(1, primal, dres)
-    with scope("sums_z"):
-        forward_sums(1)
-    with scope("sums_x"):
-        factor2 = factor_of(1, penalty)
+        primal, dres = lax.fori_loop(0, CZ, last, (zero, zero), unroll=4)
+    put_sums(1, primal, dres)
+    send_all()
+    with scope("sums"):
+        got = redall.at[pl.ds(1, GZ * BRICKS - 1)]
+        pltpu.make_async_copy(got, got, all_recv).wait()
+    factor2 = factor_from(red0[1] + jnp.sum(redall[1 : GZ * BRICKS], axis=0), penalty)
     scale = (1.0 / factor2)[0:1].reshape(1, 1, 1, CX)
-    dual_out[...] = dl[...] * scale
+    with scope("scale"):
+        dual_out[...] = dl[...] * scale
 
     with scope("wait_sends"):
         for h in hubs:
@@ -638,10 +659,12 @@
         for n in range(2):
             for i, ref in enumerate((snd1, snd2)):
                 arrivals(ref.at[n], a_send.at[n, i])
-            for t in range(1, GZ):
-                redz_copy(n, t).wait_send()
-            got = redx.at[n, pl.ds(1, BRICKS - 1)]
-            pltpu.make_async_copy(got, got, rx_send.at[n]).wait()
+        for t in range(1, GZ):
+            redz_copy(0, t).wait_send()
+        got = redx.at[0, pl.ds(1, BRICKS - 1)]
+        pltpu.make_async_copy(got, got, rx_send.at[0]).wait()
+        got = redall.at[pl.ds(1, GZ * BRICKS - 1)]
+        pltpu.make_async_copy(got, got, all_send).wait()
 
 
 def body(start, measured, tiles, tile_block, angle_row):
@@ -708,6 +731,7 @@
             vm((2, GZ, 1, CX), F32),
             vm((2, 1, CX), F32),
             vm((2, BRICKS, 1, CX), F32),
+            vm((GZ * BRICKS, 1, CX), F32),
             vm((3 * CX, CX), BF16),
             vm((96, CX), BF16),
             vm((3 * CX, CX), BF16),
@@ -726,6 +750,8 @@
             dma((2, GZ)),
             dma((2,)),
             dma((2,)),
+            dma,
+            dma,
         ],
         compiler_params=pltpu.CompilerParams(
             collective_id=0, has_side_effects=True, vmem_limit_bytes=60 * 1024 * 1024

time: 83.1 us -> 80.5 us (0.969)
  Pallas kernels: 80.8 us -> 78.1 us
    pallas_call x1, Pallas kernels: 80.8 us -> 78.1 us  [body(): pl.pallas_call(kernel, out_shape=(pltpu.VMEM((CZ, CY, CX), F32), pltpu.VM...]
where the time goes in v4:
time: 80.5 us; the launch traced here: 80.4 us
  Pallas kernels  78.1 us (97%)
  local copies, waits for them, and re-layouts  1.58 us (2%)
    pallas_call x1, Pallas kernels, body(): pl.pallas_call(kernel, out_shape=(pltpu.VMEM((CZ, CY, CX), F32), pltpu.VM...  78.1 us

profile of v4, /device:TPU:1, one launch (start us, length us, event | category | flops | bytes accessed | tf_op | source)
XLA Modules:
  0.0 80.4 jit_solution(15530556692560560354)
XLA Ops:
  0.6 78.1 %shard_map.68 = (f32[32,16,128]{2,1,0:T(8,128)S(1)}, f32[3,32,16,128]{3,2,1,0:T(8,128)S(1)}) custom-call(f32[32,16,128]{2,1,0:T(8,128)} %start_ref.1, f32[1,8,1024]{2,1,0:T(8,128)} %meas_ref.1, bf16[2048,8,256]{2,1,0:T(8,128)(2,1)} %tiles_ref.1, s32[4,8,8]{2,1,0:T(8,128)} %tb_ref.1, s32[8]{0:T(128)} %row_ref.1), custom_call_target="tpu_custom_call" | custom-call | tf_op jit(solution)/shard_map/pallas_call | solution.py:674
  78.8 0.7 copy.9
  79.5 0.9 %copy.10 = f32[3,32,16,128]{3,2,1,0:T(8,128)} copy(f32[3,32,16,128]{3,2,1,0:T(8,128)S(1)} %get-tuple-element.3) | data formatting | bytes 1572864

commit v5 on v4

--- a/solution.py
+++ b/solution.py
@@ -26,7 +26,9 @@
     ((dx, dz, dc) for dz in range(4) for dx in range(4) for dc in range(2) if dx or dz or dc),
     key=lambda s: -(min(s[0], 4 - s[0]) + min(s[1], 4 - s[1])),
 )
-SPLIT = 5
+LOAD = 512
+PITCH = 9
+SPLIT = 4
 ORDER_ALL = sorted(
     ((dy, t) for dy in range(GZ) for t in range(GY * GX) if dy or t),
     key=lambda s: -(
@@ -96,12 +98,9 @@
         c.start()
 
     def tile_copy(c):
-        rows = pl.ds(pl.multiple_of(c * CHUNK, CHUNK), CHUNK)
+        rows = pl.ds(c * LOAD, LOAD)
         return pltpu.make_async_copy(tiles_ref.at[rows], raw.at[rows], tile_sem.at[c])
 
-    @pl.loop(0, NCHUNK)
-    def _(c):
-        tile_copy(c).start()
 
     def there(dz, dy, dx):
         ok = True
@@ -112,7 +111,8 @@
         return ok
 
     class Hub:
-        def __init__(self, items):
+        def __init__(self, items, before=None):
+            self.before = before
             self.items = [
                 (
                     there(*d),
@@ -134,6 +134,8 @@
                     dst[...] = jnp.zeros(dst.shape, dst.dtype)
 
         def start(self):
+            if self.before is not None:
+                self.before.wait_send()
             for leaves, _, copy, _ in self.items:
                 pl.when(leaves)(copy.start)
 
@@ -152,33 +154,48 @@
             (unit, src.at[1], dst.at[0], send.at[1], recv.at[1]),
         ]
 
-    def around(m, low, high, into_low, into_high):
+    def around(m, k, low, high, into_low, into_high, before):
         items = [
-            ((0, -1, 0), low, into_high, yx_send.at[m, 0], yx_recv.at[m, 0]),
-            ((0, 1, 0), high, into_low, yx_send.at[m, 1], yx_recv.at[m, 1]),
+            ((0, -1, 0), low, into_high, yx_send.at[0], yx_recv.at[k, 0]),
+            ((0, 1, 0), high, into_low, yx_send.at[1], yx_recv.at[k, 1]),
         ]
-        k = 2
+        i = 2
         for sy in (0, -1, 1):
             for side, sx in ((0, -1), (1, 1)):
                 items.append((
                     (0, sy, sx), xs.at[m, side], xr.at[m, 1 - sy, 1 - side],
-                    yx_send.at[m, k], yx_recv.at[m, k],
+                    yx_send.at[i], yx_recv.at[k, i],
                 ))
-                k += 1
-        return Hub(items)
-
-    zhub = [Hub(pair(0, zs.at[n], zr.at[n], z_send.at[n], z_recv.at[n])) for n in range(3)]
-    zhub2 = Hub(pair(0, zs2, zr2, z_send.at[3], z_recv.at[3]))
-    yxhub = [around(n, ys.at[n, 0], ys.at[n, 1], yr.at[n, 0], yr.at[n, 1]) for n in range(4)]
-    yxhub2 = around(4, ys2, ys2, yr2.at[0], yr2.at[1])
-    fhub = [
-        Hub(
-            pair(0, fzs.at[n], fzr.at[n], f_send.at[n, 0], f_recv.at[n, 0])
-            + pair(1, fys.at[n], fyr.at[n], f_send.at[n, 1], f_recv.at[n, 1])
-            + pair(2, fxs.at[n], fxr.at[n], f_send.at[n, 2], f_recv.at[n, 2])
+                i += 1
+        return Hub(items, before)
+
+    def zswap(k, src, dst, before):
+        return Hub(pair(0, src, dst, z_send, z_recv.at[k]), before)
+
+    zhub = [zswap(0, zs.at[0], zr.at[0], None)]
+    zhub.append(zswap(1, zs.at[1], zr.at[1], zhub[0]))
+    zhub2 = zswap(0, zs2, zr2, zhub[1])
+    zhub.append(zswap(1, zs.at[2], zr.at[2], zhub2))
+
+    def yxswap(n, k, before):
+        return around(n, k, ys.at[n, 0], ys.at[n, 1], yr.at[n, 0], yr.at[n, 1], before)
+
+    yxhub = [yxswap(0, 0, None)]
+    yxhub.append(yxswap(1, 1, yxhub[0]))
+    yxhub2 = around(4, 0, ys2, ys2, yr2.at[0], yr2.at[1], yxhub[1])
+    yxhub.append(yxswap(2, 1, yxhub2))
+    yxhub.append(yxswap(3, 0, yxhub[2]))
+    fhub = []
+    for n in range(3):
+        k = n % 2
+        fhub.append(
+            Hub(
+                pair(0, fzs.at[n], fzr.at[n], f_send.at[0], f_recv.at[k, 0])
+                + pair(1, fys.at[n], fyr.at[n], f_send.at[1], f_recv.at[k, 1])
+                + pair(2, fxs.at[n], fxr.at[n], f_send.at[2], f_recv.at[k, 2]),
+                fhub[-1] if n else None,
+            )
         )
-        for n in range(3)
-    ]
     hubs = zhub + [zhub2] + yxhub + [yxhub2] + fhub
     for h in hubs:
         h.clear()
@@ -218,20 +235,26 @@
             tbv[b * GX + c] = rows[:, c * CX : (c + 1) * CX]
 
     def relayout(low, high):
+        for c in range(V // LOAD):
+            if low * CHUNK <= c * LOAD < high * CHUNK:
+                tile_copy(c).wait()
+
         @pl.loop(low, high)
         def _(c):
-            tile_copy(c).wait()
             rows = pl.ds(pl.multiple_of(c * CHUNK, CHUNK), CHUNK)
-            block = raw[rows].astype(F32).reshape(CHUNK * ANG, DW)
+            block = raw[rows].astype(F32)
             for h in range(2):
-                tmp[h] = block[:, h * 128 : (h + 1) * 128]
+                for j in range(CHUNK):
+                    tmp[h, PITCH * j : PITCH * j + ANG, :] = block[j, :, h * 128 : (h + 1) * 128]
             for a in range(ANG):
                 for h in range(2):
-                    part = tmp[h, pl.ds(a, CHUNK, stride=ANG), :]
+                    part = tmp[h, pl.ds(a, CHUNK, stride=PITCH), :]
                     mat[rows, a * DW + h * 128 : a * DW + (h + 1) * 128] = part.astype(BF16)
 
-    for c in ld:
-        c.wait()
+    ld[0].wait()
+    for c in range(V // LOAD):
+        tile_copy(c).start()
+    ld[1].wait()
     for a in range(ANG):
         acc[pl.ds(a, 1), :] = obs[0, pl.ds(row_ref[a], 1), :]
 
@@ -344,13 +367,13 @@
 
     def redz_copy(n, t):
         return pltpu.make_async_remote_copy(
-            red0.at[n], redz.at[n, t], rz_send.at[n, t], rz_recv.at[n, t],
+            red0.at[n], redz.at[n, t], rz_send, rz_recv,
             device_id=(lax.rem(gz + t, GZ), gy, gx), device_id_type=MESH,
         )
 
     def redx_copy(n, t):
         return pltpu.make_async_remote_copy(
-            red1.at[n], redx.at[n, t], rx_send.at[n], rx_recv.at[n],
+            red1.at[n], redx.at[n, t], rx_send, rx_recv,
             device_id=member(t)[1], device_id_type=MESH,
         )
 
@@ -368,11 +391,9 @@
             ).start()
 
     def forward_sums(n):
-        total = red0[n]
-        for t in range(1, GZ):
-            redz_copy(n, t).wait_recv()
-            total += redz[n, t]
-        red1[n] = total
+        got = redz.at[n, pl.ds(1, GZ - 1)]
+        pltpu.make_async_copy(got, got, rz_recv).wait()
+        red1[n] = red0[n] + jnp.sum(redz[n, 1:GZ], axis=0)
 
         for t in range(1, BRICKS):
             redx_copy(n, t).start()
@@ -380,7 +401,7 @@
     def factor_of(n, penalty):
         total = red1[n]
         got = redx.at[n, pl.ds(1, BRICKS - 1)]
-        pltpu.make_async_copy(got, got, rx_recv.at[n]).wait()
+        pltpu.make_async_copy(got, got, rx_recv).wait()
         total += jnp.sum(redx[n, 1:BRICKS], axis=0)
         return factor_from(total, penalty)
 
@@ -394,9 +415,12 @@
         got = ref.at[pl.ds(0, BRICKS - 1)]
         pltpu.make_async_copy(got, got, sem).wait()
 
+    def sent(n, ref):
+        arrivals(ref.at[n], a_send)
+
     def send_block(n, i, src, dst, d, dev):
         pltpu.make_async_remote_copy(
-            src.at[n, d], dst.at[n, me], a_send.at[n, i], a_recv.at[n, i],
+            src.at[n, d], dst.at[n, me], a_send, a_recv.at[n, i],
             device_id=dev, device_id_type=MESH,
         ).start()
 
@@ -414,6 +438,8 @@
             rows = pl.ds(pl.multiple_of(d * ANG, ANG), ANG)
             return jnp.concatenate([stage[0, rows, :], stage[1, rows, :]], axis=1).astype(BF16)
 
+        if n:
+            sent(0, snd2)
         for t in range(1, BRICKS):
             d, dev = member(t)
             snd1[n, d] = block_of(d)
@@ -446,6 +472,7 @@
                 c = jnp.where(t == float(q), mis[:, q * DW : (q + 1) * DW], c)
             return c.astype(BF16)
 
+        sent(n, snd1)
         for t in range(1, BRICKS):
             d, dev = member(t)
             snd2[n, d] = chosen(d)
@@ -654,15 +681,13 @@
         dual_out[...] = dl[...] * scale
 
     with scope("wait_sends"):
-        for h in hubs:
+        for h in (zhub[2], yxhub[3], fhub[2]):
             h.wait_send()
-        for n in range(2):
-            for i, ref in enumerate((snd1, snd2)):
-                arrivals(ref.at[n], a_send.at[n, i])
-        for t in range(1, GZ):
-            redz_copy(0, t).wait_send()
+        sent(1, snd2)
+        got = redz.at[0, pl.ds(1, GZ - 1)]
+        pltpu.make_async_copy(got, got, rz_send).wait()
         got = redx.at[0, pl.ds(1, BRICKS - 1)]
-        pltpu.make_async_copy(got, got, rx_send.at[0]).wait()
+        pltpu.make_async_copy(got, got, rx_send).wait()
         got = redall.at[pl.ds(1, GZ * BRICKS - 1)]
         pltpu.make_async_copy(got, got, all_send).wait()
 
@@ -688,7 +713,7 @@
         scratch_shapes=[
             vm((V, ANG, DW), BF16),
             vm((V, ANG * DW), BF16),
-            vm((2, CHUNK * ANG, 128), F32),
+            vm((2, CHUNK * PITCH, 128), F32),
             block, block, block,
             vm((ROWS, CX), F32),
             block,
@@ -737,19 +762,19 @@
             vm((3 * CX, CX), BF16),
             vm((64, CX), BF16),
             dma((2,)),
-            dma((NCHUNK,)),
-            dma((4, 2)),
-            dma((4, 2)),
-            dma((5, 8)),
-            dma((5, 8)),
-            dma((3, 3, 2)),
-            dma((3, 3, 2)),
+            dma((V // LOAD,)),
+            dma((2,)),
             dma((2, 2)),
+            dma((8,)),
+            dma((2, 8)),
+            dma((3, 2)),
+            dma((2, 3, 2)),
+            dma,
             dma((2, 2)),
-            dma((2, GZ)),
-            dma((2, GZ)),
-            dma((2,)),
-            dma((2,)),
+            dma,
+            dma,
+            dma,
+            dma,
             dma,
             dma,
         ],

time: 80.5 us -> 79.4 us (0.986)
  Pallas kernels: 78.1 us -> 77 us
    pallas_call x1, Pallas kernels: 78.1 us -> 77 us  [body(): pl.pallas_call(kernel, out_shape=(pltpu.VMEM((CZ, CY, CX), F32), pltpu.VM...]
where the time goes in v5:
time: 79.4 us; the launch traced here: 79.2 us
  Pallas kernels  77 us (97%)
  local copies, waits for them, and re-layouts  1.58 us (2%)
    pallas_call x1, Pallas kernels, body(): pl.pallas_call(kernel, out_shape=(pltpu.VMEM((CZ, CY, CX), F32), pltpu.VM...  77 us

profile of v5, /device:TPU:1, one launch (start us, length us, event | category | flops | bytes accessed | tf_op | source)
XLA Modules:
  0.0 79.2 jit_solution(17733787509201929357)
XLA Ops:
  0.6 77.0 %shard_map.68 = (f32[32,16,128]{2,1,0:T(8,128)S(1)}, f32[3,32,16,128]{3,2,1,0:T(8,128)S(1)}) custom-call(f32[32,16,128]{2,1,0:T(8,128)} %start_ref.1, f32[1,8,1024]{2,1,0:T(8,128)} %meas_ref.1, bf16[2048,8,256]{2,1,0:T(8,128)(2,1)} %tiles_ref.1, s32[4,8,8]{2,1,0:T(8,128)} %tb_ref.1, s32[8]{0:T(128)} %row_ref.1), custom_call_target="tpu_custom_call" | custom-call | tf_op jit(solution)/shard_map/pallas_call | solution.py:699
  77.6 0.7 copy.9
  78.3 0.9 %copy.10 = f32[3,32,16,128]{3,2,1,0:T(8,128)} copy(f32[3,32,16,128]{3,2,1,0:T(8,128)S(1)} %get-tuple-element.3) | data formatting | bytes 1572864

commit v6 on v5

--- a/solution.py
+++ b/solution.py
@@ -27,6 +27,8 @@
     key=lambda s: -(min(s[0], 4 - s[0]) + min(s[1], 4 - s[1])),
 )
 LOAD = 512
+ROWS9 = (CZ + 2) * CY
+ROWS9P = -(-ROWS9 // 128) * 128
 PITCH = 9
 SPLIT = 4
 ORDER_ALL = sorted(
@@ -56,11 +58,12 @@
     x_out, dual_out,
     raw, mat, tmp, x0, w1, w2, res, qbuf, xa, zbuf, zmid, ybuf, ymid, tbv, obs, mis, acc,
     zs, zr, zs2, zr2, ys, yr, ys2, yr2, xs, xr,
-    fzs, fzr, fys, fyr, fxs, fxr,
+    zs9, zr9, ys9, yr9, xs9, xr9,
+    fzs, fzr, fys, fyr, fxs, fxr, fzs2, fzr2, fys2, fyr2, fxs2, fxr2, fz2, fy2,
     stage, sl, snd1, rcv1, snd2, rcv2,
     hterm, back, dl, dlm, xlr, bdl,
     red0, redz, red1, redx, redall,
-    bx, wx, bx2, wx2,
+    bx, wx, bx2, wx2, bx9, wx9,
     load_sem, tile_sem, z_send, z_recv, yx_send, yx_recv, f_send, f_recv,
     a_send, a_recv, rz_send, rz_recv, rx_send, rx_recv, all_send, all_recv,
 ):
@@ -154,7 +157,7 @@
             (unit, src.at[1], dst.at[0], send.at[1], recv.at[1]),
         ]
 
-    def around(m, k, low, high, into_low, into_high, before):
+    def around(k, low, high, into_low, into_high, faces, halos, before):
         items = [
             ((0, -1, 0), low, into_high, yx_send.at[0], yx_recv.at[k, 0]),
             ((0, 1, 0), high, into_low, yx_send.at[1], yx_recv.at[k, 1]),
@@ -163,7 +166,7 @@
         for sy in (0, -1, 1):
             for side, sx in ((0, -1), (1, 1)):
                 items.append((
-                    (0, sy, sx), xs.at[m, side], xr.at[m, 1 - sy, 1 - side],
+                    (0, sy, sx), faces.at[side], halos.at[1 - sy, 1 - side],
                     yx_send.at[i], yx_recv.at[k, i],
                 ))
                 i += 1
@@ -175,27 +178,34 @@
     zhub = [zswap(0, zs.at[0], zr.at[0], None)]
     zhub.append(zswap(1, zs.at[1], zr.at[1], zhub[0]))
     zhub2 = zswap(0, zs2, zr2, zhub[1])
-    zhub.append(zswap(1, zs.at[2], zr.at[2], zhub2))
+    zhub.append(zswap(1, zs9, zr9, zhub2))
 
     def yxswap(n, k, before):
-        return around(n, k, ys.at[n, 0], ys.at[n, 1], yr.at[n, 0], yr.at[n, 1], before)
+        low, high = yr.at[n, 0], yr.at[n, 1]
+        return around(k, ys.at[n, 0], ys.at[n, 1], low, high, xs.at[n], xr.at[n], before)
 
     yxhub = [yxswap(0, 0, None)]
     yxhub.append(yxswap(1, 1, yxhub[0]))
-    yxhub2 = around(4, 0, ys2, ys2, yr2.at[0], yr2.at[1], yxhub[1])
+    yxhub2 = around(0, ys2, ys2, yr2.at[0], yr2.at[1], xs.at[3], xr.at[3], yxhub[1])
     yxhub.append(yxswap(2, 1, yxhub2))
-    yxhub.append(yxswap(3, 0, yxhub[2]))
+    yxhub.append(
+        around(0, ys9.at[0], ys9.at[1], yr9.at[0], yr9.at[1], xs9, xr9, yxhub[2])
+    )
     fhub = []
-    for n in range(3):
-        k = n % 2
+    for k, z, y, x in (
+        (0, (fzs.at[0], fzr.at[0]), (fys.at[0], fyr.at[0]), (fxs.at[0], fxr.at[0])),
+        (1, (fzs.at[1], fzr.at[1]), (fys.at[1], fyr.at[1]), (fxs.at[1], fxr.at[1])),
+        (0, (fzs2, fzr2), (fys2, fyr2), (fxs2, fxr2)),
+    ):
         fhub.append(
             Hub(
-                pair(0, fzs.at[n], fzr.at[n], f_send.at[0], f_recv.at[k, 0])
-                + pair(1, fys.at[n], fyr.at[n], f_send.at[1], f_recv.at[k, 1])
-                + pair(2, fxs.at[n], fxr.at[n], f_send.at[2], f_recv.at[k, 2]),
-                fhub[-1] if n else None,
+                pair(0, *z, f_send.at[0], f_recv.at[k, 0])
+                + pair(1, *y, f_send.at[1], f_recv.at[k, 1])
+                + pair(2, *x, f_send.at[2], f_recv.at[k, 2]),
+                fhub[-1] if fhub else None,
             )
         )
+    xs9[...] = jnp.zeros_like(xs9)
     hubs = zhub + [zhub2] + yxhub + [yxhub2] + fhub
     for h in hubs:
         h.clear()
@@ -227,6 +237,22 @@
     pick = jnp.where(s1 == want, 1.0, 0.0).astype(BF16)
     pick2 = jnp.where(k1 == jnp.where(k0 < 16, k0, CX - 32 + k0), 1.0, 0.0).astype(BF16)
 
+    def place(c):
+        edge = jnp.where(c == CX, -1, jnp.where(c == 2 * CX - 1, CX, 4 * CX))
+        return jnp.where(c < CX, c, edge)
+
+    def last_weights():
+        shape = (CX, 2 * CX)
+        hi, lo = split(gauss(iota(shape, 0) - place(iota(shape, 1))))
+        bx9[0:CX] = hi
+        bx9[CX : 2 * CX] = hi
+        bx9[2 * CX : 3 * CX] = lo
+        shape = (32, 2 * CX)
+        k = iota(shape, 0)
+        hi, lo = split(gauss(jnp.where(k < 16, k - 16, CX - 16 + k) - place(iota(shape, 1))))
+        wx9[0:32] = hi
+        wx9[32:64] = lo
+
     wide = (GX, GX * CX)
     spread = jnp.where(iota(wide, 0) == iota(wide, 1) // CX, 1.0, 0.0).astype(BF16)
     for b in range(GY):
@@ -272,6 +298,19 @@
         fxs[n, 0] = f[0:16]
         fxs[n, 1] = f[16:32]
         fhub[n].start()
+
+    def send_terms():
+        for i, src in enumerate((hterm, bdl)):
+            fzs2[0, i] = src[0]
+            fzs2[1, i] = src[CZ - 1]
+            v = src[...]
+            fys2[0, i] = v[:, 0, :]
+            fys2[1, i] = v[:, CY - 1, :]
+            hi, lo = split(v.reshape(ROWS, CX))
+            f = dot(pick, jnp.concatenate([hi, lo], axis=1), ((1,), (1,))).astype(BF16)
+            fxs2[0, i] = f[0:16]
+            fxs2[1, i] = f[16:32]
+        fhub[2].start()
 
     def send_z(n, src):
         zs[n, 0] = src[0:R].reshape(R * CY, CX).astype(BF16)
@@ -341,15 +380,15 @@
         xa[0] = fzr[n, 0]
         xa[CZ + 1] = fzr[n, 1]
 
-    def diffs(n, z):
+    def diffs(fy, z):
         v = xa[z + 1]
         up, low = xa[z + 2], xa[z]
         yield (
             jnp.where((z == CZ - 1) & ends[0][1], 0.0, up - v),
             jnp.where((z == 0) & ends[0][0], 0.0, v - low),
         )
-        up = jnp.where(sub == CY - 1, fyr[n, 1, pl.ds(z, 1), :], pltpu.roll(v, CY - 1, 0))
-        low = jnp.where(sub == 0, fyr[n, 0, pl.ds(z, 1), :], pltpu.roll(v, 1, 0))
+        up = jnp.where(sub == CY - 1, fy[1, pl.ds(z, 1), :], pltpu.roll(v, CY - 1, 0))
+        low = jnp.where(sub == 0, fy[0, pl.ds(z, 1), :], pltpu.roll(v, 1, 0))
         yield (
             jnp.where((sub == CY - 1) & ends[1][1], 0.0, up - v),
             jnp.where((sub == 0) & ends[1][0], 0.0, v - low),
@@ -516,7 +555,7 @@
     def _(z):
         smooth = jnp.zeros((CY, CX), F32)
         shrunk = jnp.zeros((CY, CX), F32)
-        for j, jm in diffs(0, z):
+        for j, jm in diffs(fyr.at[0], z):
             s = j - jnp.clip(j, -cut, cut)
             sm = jm - jnp.clip(jm, -cut, cut)
             smooth += jm - j
@@ -544,6 +583,7 @@
     whi, wlo = split(twice[CX : CX + 32])
     wx2[0:32] = whi
     wx2[32:64] = wlo
+    last_weights()
 
     return_misfit(0)
     blur_z(1, x0, w1)
@@ -572,21 +612,21 @@
     hi = w2[...].reshape(ROWS, CX).astype(BF16)
     ys2[...] = hi
     f = dot(pick2, hi, ((1,), (1,))).astype(BF16)
-    xs[4, 0] = f[0:16]
-    xs[4, 1] = f[16:32]
+    xs[3, 0] = f[0:16]
+    xs[3, 1] = f[16:32]
     yxhub2.start()
     w1[...] = zmid[8 : 8 + CZ]
 
-    ymid[:, 16 : 16 + CY, :] = own_rows(w2, bx2).reshape(CZ, CY, CX)
+    ymid[0:CZ, 16 : 16 + CY, :] = own_rows(w2, bx2).reshape(CZ, CY, CX)
     with scope("wait_yx2"):
         yxhub2.wait_recv()
     send_yx(2, w1)
-    ymid[:, 16 : 16 + CY, :] += rows_of(4, 1, wx2[...]).reshape(CZ, CY, CX)
+    ymid[0:CZ, 16 : 16 + CY, :] += rows_of(3, 1, wx2[...]).reshape(CZ, CY, CX)
     for side in range(2):
         y = yr2[side]
         rows = dot(jnp.concatenate([y, y], axis=1), bx2[CX:], ((1,), (0,)))
-        rows = rows + rows_of(4, 2 * side, wx2[...])
-        ymid[:, 32 * side : 32 * side + 16, :] = rows.reshape(CZ, CY, CX)
+        rows = rows + rows_of(3, 2 * side, wx2[...])
+        ymid[0:CZ, 32 * side : 32 * side + 16, :] = rows.reshape(CZ, CY, CX)
     sub2 = iota((CY + 16, CX), 0)
     outside = ((sub2 < 8) & ends[1][0]) | ((sub2 >= CY + 8) & ends[1][1])
 
@@ -612,7 +652,7 @@
         smooth = jnp.zeros((CY, CX), F32)
         shrunk = jnp.zeros((CY, CX), F32)
         bdual = jnp.zeros((CY, CX), F32)
-        for axis, (j, jm) in enumerate(diffs(1, z)):
+        for axis, (j, jm) in enumerate(diffs(fyr.at[1], z)):
             s = j - jnp.clip(j, -cut, cut)
             sm = jm - jnp.clip(jm, -cut, cut)
             d = j - s
@@ -634,30 +674,99 @@
     put_sums(0, primal, dres)
     for t in range(1, GZ):
         redz_copy(0, t).start()
+    send_terms()
     backproject(1, w2)
-    send_z(2, w2)
+    zs9[0] = w2[0 : R + 1].reshape((R + 1) * CY, CX).astype(BF16)
+    zs9[1] = w2[CZ - R - 1 : CZ].reshape((R + 1) * CY, CX).astype(BF16)
+    zhub[2].start()
     forward_sums(0)
-    blur_z(2, w2, w1)
-    send_yx(3, w1)
+    zbuf[R + 1 : R + 1 + CZ] = w2[...]
+    with scope("wait_z"):
+        zhub[2].wait_recv()
+    zbuf[0 : R + 1] = zr9[0].astype(F32).reshape(R + 1, CY, CX)
+    zbuf[R + 1 + CZ : 2 * R + 2 + CZ] = zr9[1].astype(F32).reshape(R + 1, CY, CX)
+
+    @pl.loop(0, CZ + 2, unroll=2)
+    def _(z):
+        zmid[z] = taps(lambda k: zbuf[z + k])
+
+    outer = zmid[0 : CZ + 2]
+    n9 = (CZ + 2) * R
+    for side, at, ninth in ((0, slice(0, R), R), (1, slice(CY - R, CY), CY - R - 1)):
+        ys9[side, 0:n9] = outer[:, at, :].reshape(n9, CX).astype(BF16)
+        ys9[side, n9:] = outer[1 : CZ + 1, ninth, :].astype(BF16)
+    hi, lo = split(outer.reshape(ROWS9, CX))
+    f = dot(pick2, hi, ((1,), (1,))).astype(BF16)
+    xs9[0, :, 0:ROWS9] = f[0:16]
+    xs9[1, :, 0:ROWS9] = f[16:32]
+    yxhub[3].start()
+    both = jnp.concatenate([hi, lo], axis=1)
+    own = dot(both, bx9[0 : 2 * CX], ((1,), (0,))) + dot(hi, bx9[2 * CX :], ((1,), (0,)))
+    own = own.reshape(CZ + 2, CY, 2 * CX)
+    ymid[0 : CZ + 2, 16 : 16 + CY, :] = own[:, :, 0:CX]
+    ybuf[:, R : R + CY, :] = own[1 : CZ + 1, :, CX:]
     penalty = factor_of(0, jnp.ones((8, CX), F32))
     inv1 = 1.0 / penalty
     pen3 = penalty[0:1].reshape(1, 1, CX)
     inv3 = inv1[0:1].reshape(1, 1, CX)
-    x0[...] = x0[...] - STEP * pen3 * (hterm[...] + bdl[...] * inv3)
+    spen = STEP * pen3
+    x0[...] = x0[...] - spen * (hterm[...] + bdl[...] * inv3)
     dl[...] = dl[...] * inv3
     dlm[...] = dlm[...] * inv3
-    blur_yx(3, w1, w2)
-    x0[...] = x0[...] - STEP * w2[...]
-    send_faces(2, x0)
-    x_out[...] = x0[...]
-    xa[1 : CZ + 1] = x0[...]
-    wait_faces(2)
+    with scope("wait_terms"):
+        fhub[2].wait_recv()
+    for side in range(2):
+        fz2[side] = fzr[1, side] - spen[0] * (fzr2[side, 0] + fzr2[side, 1] * inv3[0])
+        fy2[side] = fyr[1, side] - spen[0] * (fyr2[side, 0] + fyr2[side, 1] * inv3[0])
+    rims = [
+        dot(
+            jnp.concatenate([fxr2[0, i], fxr2[1, i]], axis=0), wx[64:96], ((0,), (0,))
+        ).reshape(CZ, CY, CX)
+        for i in range(2)
+    ]
+    xlr[...] = xlr[...] - spen * (rims[0] + rims[1] * inv3)
+
+    def halo_rows(slot):
+        h = xr9[slot].reshape(32, ROWS9P)[:, 0:ROWS9]
+        h = dot(jnp.concatenate([h, h], axis=0), wx9[...], ((0,), (0,)))
+        return h.reshape(CZ + 2, CY, 2 * CX)
+
+    with scope("wait_yx"):
+        yxhub[3].wait_recv()
+    more = halo_rows(1)
+    ymid[0 : CZ + 2, 16 : 16 + CY, :] += more[:, :, 0:CX]
+    ybuf[:, R : R + CY, :] += more[1 : CZ + 1, :, CX:]
+    for side, at, ninth in ((0, slice(CY - R, CY), CY - R - 1), (1, slice(0, R), R)):
+        y = yr9[side]
+        rows = dot(jnp.concatenate([y, y], axis=1), bx9[CX:], ((1,), (0,)))
+        more = halo_rows(2 * side)
+        near = rows[0:n9].reshape(CZ + 2, R, 2 * CX) + more[:, at, :]
+        far = rows[n9:, 0:CX] + more[1 : CZ + 1, ninth, 0:CX]
+        to = slice(16 - R, 16) if side == 0 else slice(16 + CY, 16 + CY + R)
+        ymid[0 : CZ + 2, to, :] = near[:, :, 0:CX]
+        ymid[1 : CZ + 1, (15 - R if side == 0 else 16 + CY + R), :] = far
+        to = slice(0, R) if side == 0 else slice(R + CY, 2 * R + CY)
+        ybuf[:, to, :] = near[1 : CZ + 1, :, CX:]
+
+    @pl.loop(0, CZ, unroll=2)
+    def _(z):
+        v = x0[z] - STEP * taps(lambda k: ymid[z + 1, 16 - R + k : 16 - R + CY + k, :])
+        xa[z + 1] = v
+        x_out[z] = v
+        xlr[z] = xlr[z] - STEP * taps(lambda k: ybuf[z, k : k + CY, :])
+        low = taps(lambda k: ymid[z + 1, k : k + R, :])[R - 1 : R]
+        fy2[0, pl.ds(z, 1), :] = fy2[0, pl.ds(z, 1), :] - STEP * low
+        high = taps(lambda k: ymid[z + 1, 16 + R + k : 16 + 2 * R + k, :])[0:1]
+        fy2[1, pl.ds(z, 1), :] = fy2[1, pl.ds(z, 1), :] - STEP * high
+
+    for side, at in ((0, 0), (1, CZ + 1)):
+        xa[at] = fz2[side] - STEP * taps(lambda k: ymid[at, 16 - R + k : 16 - R + CY + k, :])
     cut2 = (SHRINK / penalty)[0:1]
 
     def last(z, sums):
         primal, dres = sums
         shrunk = jnp.zeros((CY, CX), F32)
-        for axis, (j, jm) in enumerate(diffs(2, z)):
+        for axis, (j, jm) in enumerate(diffs(fy2, z)):
             t = j + dl[axis, z]
             tm = jm + dlm[axis, z]
             s = t - jnp.clip(t, -cut2, cut2)
@@ -721,27 +830,41 @@
             vm((CZ + 32, CY, CX), F32),
             vm((CZ + 16, CY, CX), F32),
             vm((CZ, CY + 16, CX), F32),
-            vm((CZ, CY + 32, CX), F32),
+            vm((CZ + 2, CY + 32, CX), F32),
             vm((BRICKS, ANG, CX), F32),
             vm((1, ANG, NBLK * DW), F32),
             vm((ANG, NBLK * DW), F32),
             vm((ANG, NBLK * DW), F32),
-            vm((3, 2, R * CY, CX), BF16),
-            vm((3, 2, R * CY, CX), BF16),
+            vm((2, 2, R * CY, CX), BF16),
+            vm((2, 2, R * CY, CX), BF16),
             vm((2, 16 * CY, CX), BF16),
             vm((2, 16 * CY, CX), BF16),
-            vm((4, 2, CZ * R, CX), BF16),
-            vm((4, 2, CZ * R, CX), BF16),
+            vm((3, 2, CZ * R, CX), BF16),
+            vm((3, 2, CZ * R, CX), BF16),
             vm((ROWS, CX), BF16),
             vm((2, ROWS, CX), BF16),
-            vm((5, 2, 16, ROWS), BF16),
-            vm((5, 3, 2, 16, ROWS), BF16),
-            vm((3, 2, CY, CX), F32),
-            vm((3, 2, CY, CX), F32),
-            vm((3, 2, CZ, CX), F32),
-            vm((3, 2, CZ, CX), F32),
-            vm((3, 2, 16, ROWS), BF16),
-            vm((3, 2, 16, ROWS), BF16),
+            vm((4, 2, 16, ROWS), BF16),
+            vm((4, 3, 2, 16, ROWS), BF16),
+            vm((2, (R + 1) * CY, CX), BF16),
+            vm((2, (R + 1) * CY, CX), BF16),
+            vm((2, (CZ + 2) * R + CZ, CX), BF16),
+            vm((2, (CZ + 2) * R + CZ, CX), BF16),
+            vm((2, 16, ROWS9P), BF16),
+            vm((3, 2, 16, ROWS9P), BF16),
+            vm((2, 2, CY, CX), F32),
+            vm((2, 2, CY, CX), F32),
+            vm((2, 2, CZ, CX), F32),
+            vm((2, 2, CZ, CX), F32),
+            vm((2, 2, 16, ROWS), BF16),
+            vm((2, 2, 16, ROWS), BF16),
+            vm((2, 2, CY, CX), F32),
+            vm((2, 2, CY, CX), F32),
+            vm((2, 2, CZ, CX), F32),
+            vm((2, 2, CZ, CX), F32),
+            vm((2, 2, 16, ROWS), BF16),
+            vm((2, 2, 16, ROWS), BF16),
+            vm((2, CY, CX), F32),
+            vm((2, CZ, CX), F32),
             vm((2, CZ * ANG, 128), F32),
             vm((CZ, V), BF16),
             vm((2, BRICKS, ANG, DW), BF16),
@@ -761,6 +884,8 @@
             vm((96, CX), BF16),
             vm((3 * CX, CX), BF16),
             vm((64, CX), BF16),
+            vm((3 * CX, 2 * CX), BF16),
+            vm((64, 2 * CX), BF16),
             dma((2,)),
             dma((V // LOAD,)),
             dma((2,)),

time: 79.4 us -> 76.8 us (0.967)
  Pallas kernels: 77 us -> 74.4 us
    pallas_call x1, Pallas kernels: 77 us -> 74.4 us  [body(): pl.pallas_call(kernel, out_shape=(pltpu.VMEM((CZ, CY, CX), F32), pltpu.VM...]
where the time goes in v6:
time: 76.8 us; the launch traced here: 76.7 us
  Pallas kernels  74.4 us (97%)
  local copies, waits for them, and re-layouts  1.58 us (2%)
    pallas_call x1, Pallas kernels, body(): pl.pallas_call(kernel, out_shape=(pltpu.VMEM((CZ, CY, CX), F32), pltpu.VM...  74.4 us
    unnamed x2, local copies, waits for them, and re-layouts  1.58 us

profile of v6, /device:TPU:1, one launch (start us, length us, event | category | flops | bytes accessed | tf_op | source)
XLA Modules:
  0.0 76.7 jit_solution(3050211696346448595)
XLA Ops:
  0.6 74.4 %shard_map.68 = (f32[32,16,128]{2,1,0:T(8,128)S(1)}, f32[3,32,16,128]{3,2,1,0:T(8,128)S(1)}) custom-call(f32[32,16,128]{2,1,0:T(8,128)} %start_ref.1, f32[1,8,1024]{2,1,0:T(8,128)} %meas_ref.1, bf16[2048,8,256]{2,1,0:T(8,128)(2,1)} %tiles_ref.1, s32[4,8,8]{2,1,0:T(8,128)} %tb_ref.1, s32[8]{0:T(128)} %row_ref.1), custom_call_target="tpu_custom_call" | custom-call | tf_op jit(solution)/shard_map/pallas_call | solution.py:808
  75.1 0.7 copy.9
  75.8 0.9 %copy.10 = f32[3,32,16,128]{3,2,1,0:T(8,128)} copy(f32[3,32,16,128]{3,2,1,0:T(8,128)S(1)} %get-tuple-element.3) | data formatting | bytes 1572864

commit v7 on v6

--- a/solution.py
+++ b/solution.py
@@ -57,7 +57,7 @@
     start_ref, meas_ref, tiles_ref, tb_ref, row_ref,
     x_out, dual_out,
     raw, mat, tmp, x0, w1, w2, res, qbuf, xa, zbuf, zmid, ybuf, ymid, tbv, obs, mis, acc,
-    zs, zr, zs2, zr2, ys, yr, ys2, yr2, xs, xr,
+    zs, zr, zst, tz, v1z, umid, ytwo, ys, yr, ys2, yr2, xs, xr,
     zs9, zr9, ys9, yr9, xs9, xr9,
     fzs, fzr, fys, fyr, fxs, fxr, fzs2, fzr2, fys2, fyr2, fxs2, fxr2, fz2, fy2,
     stage, sl, snd1, rcv1, snd2, rcv2,
@@ -142,8 +142,8 @@
             for leaves, _, copy, _ in self.items:
                 pl.when(leaves)(copy.start)
 
-        def wait_recv(self):
-            for _, arrives, copy, _ in self.items:
+        def wait_recv(self, part=slice(None)):
+            for _, arrives, copy, _ in self.items[part]:
                 pl.when(arrives)(copy.wait_recv)
 
         def wait_send(self):
@@ -158,18 +158,19 @@
         ]
 
     def around(k, low, high, into_low, into_high, faces, halos, before):
-        items = [
-            ((0, -1, 0), low, into_high, yx_send.at[0], yx_recv.at[k, 0]),
-            ((0, 1, 0), high, into_low, yx_send.at[1], yx_recv.at[k, 1]),
-        ]
+        items = []
         i = 2
-        for sy in (0, -1, 1):
+        for sy in (-1, 1, 0):
             for side, sx in ((0, -1), (1, 1)):
                 items.append((
                     (0, sy, sx), faces.at[side], halos.at[1 - sy, 1 - side],
                     yx_send.at[i], yx_recv.at[k, i],
                 ))
                 i += 1
+        items += [
+            ((0, -1, 0), low, into_high, yx_send.at[0], yx_recv.at[k, 0]),
+            ((0, 1, 0), high, into_low, yx_send.at[1], yx_recv.at[k, 1]),
+        ]
         return Hub(items, before)
 
     def zswap(k, src, dst, before):
@@ -177,7 +178,13 @@
 
     zhub = [zswap(0, zs.at[0], zr.at[0], None)]
     zhub.append(zswap(1, zs.at[1], zr.at[1], zhub[0]))
-    zhub2 = zswap(0, zs2, zr2, zhub[1])
+    zhub2 = Hub(
+        [
+            ((-1, 0, 0), zst.at[0:16], zst.at[80:96], z_send.at[0], z_recv.at[0, 0]),
+            ((1, 0, 0), zst.at[16:32], zst.at[64:80], z_send.at[1], z_recv.at[0, 1]),
+        ],
+        zhub[1],
+    )
     zhub.append(zswap(1, zs9, zr9, zhub2))
 
     def yxswap(n, k, before):
@@ -353,22 +360,28 @@
         both = jnp.concatenate([hi, lo], axis=1)
         return dot(both, mat3[0 : 2 * CX], ((1,), (0,))) + dot(hi, mat3[2 * CX :], ((1,), (0,)))
 
-    def blur_yx(n, w, out):
+    def blur_yx(n, w, put):
         own = own_rows(w, bx)
         ybuf[:, R : R + CY, :] = own.reshape(CZ, CY, CX)
         with scope("wait_yx"):
-            yxhub[n].wait_recv()
+            yxhub[n].wait_recv(slice(0, 6))
         ybuf[:, R : R + CY, :] += rows_of(n, 1, wx[0:64]).reshape(CZ, CY, CX)
-        for side, at in ((0, slice(CY - R, CY)), (1, slice(0, R))):
+        sides = (
+            (0, slice(CY - R, CY), slice(0, R)),
+            (1, slice(0, R), slice(R + CY, 2 * R + CY)),
+        )
+        for side, at, to in sides:
+            ybuf[:, to, :] = rows_of(n, 2 * side, wx[0:64]).reshape(CZ, CY, CX)[:, at, :]
+        with scope("wait_yx"):
+            yxhub[n].wait_recv(slice(6, 8))
+        for side, at, to in sides:
             y = yr[n, side]
             rows = dot(jnp.concatenate([y, y], axis=1), bx[CX:], ((1,), (0,)))
-            more = rows_of(n, 2 * side, wx[0:64]).reshape(CZ, CY, CX)[:, at, :]
-            to = slice(0, R) if side == 0 else slice(R + CY, 2 * R + CY)
-            ybuf[:, to, :] = rows.reshape(CZ, R, CX) + more
+            ybuf[:, to, :] += rows.reshape(CZ, R, CX)
 
         @pl.loop(0, CZ, unroll=2)
         def _(z):
-            out[z] = taps(lambda k: ybuf[z, k : k + CY, :])
+            put(z, taps(lambda k: ybuf[z, k : k + CY, :]))
 
     lane, sub = iota((CY, CX), 1), iota((CY, CX), 0)
     ends = ((gz == 0, gz == GZ - 1), (gy == 0, gy == GY - 1), (gx == 0, gx == GX - 1))
@@ -464,9 +477,6 @@
         ).start()
 
     def project(n):
-        for z0 in range(1):
-            for y in range(CY):
-                sl[:, y * CX : (y + 1) * CX] = res[pl.ds(y, CZ, stride=CY), :].astype(BF16)
         with scope("mm_fwd"):
             for a in range(ANG):
                 c = dot(sl[...], mat[:, a * DW : (a + 1) * DW], ((1,), (0,)))
@@ -519,7 +529,7 @@
 
         rcv2[n, me] = chosen(me)
 
-    def backproject(n, out):
+    def backproject(n, put):
         with scope("wait_a2"):
             arrivals(rcv2.at[n], a_recv.at[n, 1])
         r = rcv2[n].astype(F32).reshape(CZ * ANG, DW)
@@ -532,10 +542,7 @@
                 ].astype(BF16)
         with scope("mm_bwd"):
             for c in range(ANG):
-                b = dot(sl[...], mat[c * DW : (c + 1) * DW, :], ((1,), (1,)))
-                for h in range(2):
-                    res[pl.ds(2 * c + h, CZ, stride=CY), :] = b[:, h * 128 : (h + 1) * 128]
-        out[...] = res[...].reshape(CZ, CY, CX)
+                put(c, dot(sl[...], mat[c * DW : (c + 1) * DW, :], ((1,), (1,))))
 
     send_z(0, x0)
     send_faces(0, x0)
@@ -543,8 +550,13 @@
     blur_z(0, x0, w1)
     send_yx(0, w1)
     relayout(SPLIT, NCHUNK)
-    blur_yx(0, w1, w2)
-    res[...] = w2[...].reshape(ROWS, CX)
+
+    def to_res(z, v):
+        res[pl.ds(pl.multiple_of(z * CY, CY), CY), :] = v
+
+    blur_yx(0, w1, to_res)
+    for y in range(CY):
+        sl[:, y * CX : (y + 1) * CX] = res[pl.ds(y, CZ, stride=CY), :].astype(BF16)
     project(0)
 
     wait_faces(0)
@@ -585,65 +597,100 @@
     wx2[32:64] = wlo
     last_weights()
 
+    zst[96:128] = jnp.zeros((32, V), BF16)
+    shape1, shape2 = (CZ, CX), (CX, CX)
+    m = iota(shape1, 1) - 8
+    inside = ((m >= 0) | (gz > 0)) & ((m < CZ) | (gz < GZ - 1)) & (m < CZ + 8)
+    thi, tlo = split(jnp.where(inside, gauss(iota(shape1, 0) - m), 0.0))
+
+    def from_place(k):
+        halo = jnp.where(k < 80, k - 80, jnp.where(k < 96, k - 80 + CZ, 4 * CX))
+        return jnp.where(k < 64, lax.rem(k, CZ), halo)
+
+    uhi, ulo = split(gauss(iota(shape2, 0) - 8 - from_place(iota(shape2, 1))))
+    twice = (
+        dot(thi, uhi, ((1,), (0,))) + dot(thi, ulo, ((1,), (0,))) + dot(tlo, uhi, ((1,), (0,)))
+    )
+    once = gauss(iota(shape1, 0) - from_place(iota(shape1, 1)))
+    for i, t in enumerate((twice, once)):
+        hi, lo = split(t)
+        tz[32 * i : 32 * i + 32] = hi
+        tz[64 + 32 * i : 96 + 32 * i] = lo
+
     return_misfit(0)
     blur_z(1, x0, w1)
     send_yx(1, w1)
-    backproject(0, w2)
-
-    zs2[0] = w2[0:16].reshape(16 * CY, CX).astype(BF16)
-    zs2[1] = w2[CZ - 16 : CZ].reshape(16 * CY, CX).astype(BF16)
+
+    def to_stack(c, b):
+        cols = slice(c * DW, (c + 1) * DW)
+        hi, lo = split(b)
+        zst[0:32, cols] = hi
+        zst[32:64, cols] = lo
+
+    backproject(0, to_stack)
     zhub2.start()
-    blur_yx(1, w1, qbuf)
-    zbuf[16 : 16 + CZ] = w2[...]
+
+    def to_q(z, v):
+        qbuf[pl.ds(z, CY, stride=CZ), :] = v
+
+    blur_yx(1, w1, to_q)
     with scope("wait_z2"):
         zhub2.wait_recv()
-    zbuf[0:16] = zr2[0].astype(F32).reshape(16, CY, CX)
-    zbuf[16 + CZ : 32 + CZ] = zr2[1].astype(F32).reshape(16, CY, CX)
-
-    @pl.loop(0, CZ + 16, unroll=2)
-    def _(z):
-        out = ((z < 8) & ends[0][0]) | ((z >= CZ + 8) & ends[0][1])
-        zmid[z] = jnp.where(out, 0.0, taps(lambda k: zbuf[z + k]))
-
-    @pl.loop(0, CZ, unroll=2)
-    def _(z):
-        w2[z] = taps(lambda k: zmid[z + k])
-
-    hi = w2[...].reshape(ROWS, CX).astype(BF16)
+    for c in range(ANG):
+        cols = slice(c * DW, (c + 1) * DW)
+        o = dot(tz[...], zst[:, cols], ((1,), (0,)))
+        o = o[0:64] + o[64:128]
+        for h in range(2):
+            w2[ROWS // 16 * (2 * c + h) : ROWS // 16 * (2 * c + h + 1)] = o[
+                0:32, h * 128 : (h + 1) * 128
+            ]
+        v1z[:, cols] = o[32:64]
+
+    hi, lo = split(w2[...])
     ys2[...] = hi
     f = dot(pick2, hi, ((1,), (1,))).astype(BF16)
     xs[3, 0] = f[0:16]
     xs[3, 1] = f[16:32]
     yxhub2.start()
-    w1[...] = zmid[8 : 8 + CZ]
-
-    ymid[0:CZ, 16 : 16 + CY, :] = own_rows(w2, bx2).reshape(CZ, CY, CX)
+    slab = (CY, CZ, CX)
+    both = jnp.concatenate([hi, lo], axis=1)
+    own = dot(both, bx2[0 : 2 * CX], ((1,), (0,))) + dot(hi, bx2[2 * CX :], ((1,), (0,)))
+    umid[16:32] = own.reshape(slab)
+    for y in range(CY):
+        res[pl.ds(y, CZ, stride=CY), :] = v1z[:, y * CX : (y + 1) * CX]
+    w1[...] = res[...].reshape(CZ, CY, CX)
     with scope("wait_yx2"):
-        yxhub2.wait_recv()
+        yxhub2.wait_recv(slice(0, 6))
+    umid[16:32] += rows_of(3, 1, wx2[...]).reshape(slab)
+    for side in range(2):
+        umid[32 * side : 32 * side + 16] = rows_of(3, 2 * side, wx2[...]).reshape(slab)
+    with scope("wait_yx2"):
+        yxhub2.wait_recv(slice(6, 8))
     send_yx(2, w1)
-    ymid[0:CZ, 16 : 16 + CY, :] += rows_of(3, 1, wx2[...]).reshape(CZ, CY, CX)
     for side in range(2):
         y = yr2[side]
         rows = dot(jnp.concatenate([y, y], axis=1), bx2[CX:], ((1,), (0,)))
-        rows = rows + rows_of(3, 2 * side, wx2[...])
-        ymid[0:CZ, 32 * side : 32 * side + 16, :] = rows.reshape(CZ, CY, CX)
-    sub2 = iota((CY + 16, CX), 0)
-    outside = ((sub2 < 8) & ends[1][0]) | ((sub2 >= CY + 8) & ends[1][1])
-
-    @pl.loop(0, CZ, unroll=2)
-    def _(z):
-        ybuf[z] = jnp.where(outside, 0.0, taps(lambda k: ymid[z, k : k + CY + 16, :]))
-
-    @pl.loop(0, CZ, unroll=2)
-    def _(z):
-        rows = pl.ds(pl.multiple_of(z * CY, CY), CY)
-        res[rows, :] = qbuf[z] - STEP * taps(lambda k: ybuf[z, k : k + CY, :])
+        umid[32 * side : 32 * side + 16] += rows.reshape(slab)
+
+    @pl.loop(0, CY + 16)
+    def _(y):
+        out = ((y < 8) & ends[1][0]) | ((y >= CY + 8) & ends[1][1])
+        ytwo[y] = jnp.where(out, 0.0, taps(lambda k: umid[y + k]))
+
+    for y in range(CY):
+        q = qbuf[y * CZ : (y + 1) * CZ, :]
+        v = q - STEP * taps(lambda k: ytwo[y + k])
+        sl[:, y * CX : (y + 1) * CX] = v.astype(BF16)
 
     project(1)
-    blur_yx(2, w1, w2)
-    x0[...] = x0[...] - STEP * w2[...]
+
+    def to_x(z, v):
+        x = x0[z] - STEP * v
+        x0[z] = x
+        xa[z + 1] = x
+
+    blur_yx(2, w1, to_x)
     send_faces(1, x0)
-    xa[1 : CZ + 1] = x0[...]
     return_misfit(1)
     wait_faces(1)
 
@@ -675,12 +722,17 @@
     for t in range(1, GZ):
         redz_copy(0, t).start()
     send_terms()
-    backproject(1, w2)
-    zs9[0] = w2[0 : R + 1].reshape((R + 1) * CY, CX).astype(BF16)
-    zs9[1] = w2[CZ - R - 1 : CZ].reshape((R + 1) * CY, CX).astype(BF16)
+
+    def spread_rows(c, b):
+        for h in range(2):
+            res[pl.ds(2 * c + h, CZ, stride=CY), :] = b[:, h * 128 : (h + 1) * 128]
+
+    backproject(1, spread_rows)
+    zs9[0] = res[0 : (R + 1) * CY].astype(BF16)
+    zs9[1] = res[(CZ - R - 1) * CY :].astype(BF16)
     zhub[2].start()
     forward_sums(0)
-    zbuf[R + 1 : R + 1 + CZ] = w2[...]
+    zbuf[R + 1 : R + 1 + CZ] = res[...].reshape(CZ, CY, CX)
     with scope("wait_z"):
         zhub[2].wait_recv()
     zbuf[0 : R + 1] = zr9[0].astype(F32).reshape(R + 1, CY, CX)
@@ -732,21 +784,29 @@
         return h.reshape(CZ + 2, CY, 2 * CX)
 
     with scope("wait_yx"):
-        yxhub[3].wait_recv()
+        yxhub[3].wait_recv(slice(0, 6))
     more = halo_rows(1)
     ymid[0 : CZ + 2, 16 : 16 + CY, :] += more[:, :, 0:CX]
     ybuf[:, R : R + CY, :] += more[1 : CZ + 1, :, CX:]
-    for side, at, ninth in ((0, slice(CY - R, CY), CY - R - 1), (1, slice(0, R), R)):
+    sides = ((0, slice(0, 16)), (1, slice(16 + CY, 32 + CY)))
+    for side, to in sides:
+        more = halo_rows(2 * side)
+        ymid[0 : CZ + 2, to, :] = more[:, :, 0:CX]
+        if side == 0:
+            ybuf[:, 0:R, :] = more[1 : CZ + 1, CY - R :, CX:]
+        else:
+            ybuf[:, R + CY :, :] = more[1 : CZ + 1, 0:R, CX:]
+    with scope("wait_yx"):
+        yxhub[3].wait_recv(slice(6, 8))
+    for side in range(2):
         y = yr9[side]
         rows = dot(jnp.concatenate([y, y], axis=1), bx9[CX:], ((1,), (0,)))
-        more = halo_rows(2 * side)
-        near = rows[0:n9].reshape(CZ + 2, R, 2 * CX) + more[:, at, :]
-        far = rows[n9:, 0:CX] + more[1 : CZ + 1, ninth, 0:CX]
+        near = rows[0:n9].reshape(CZ + 2, R, 2 * CX)
         to = slice(16 - R, 16) if side == 0 else slice(16 + CY, 16 + CY + R)
-        ymid[0 : CZ + 2, to, :] = near[:, :, 0:CX]
-        ymid[1 : CZ + 1, (15 - R if side == 0 else 16 + CY + R), :] = far
+        ymid[0 : CZ + 2, to, :] += near[:, :, 0:CX]
+        ymid[1 : CZ + 1, (15 - R if side == 0 else 16 + CY + R), :] += rows[n9:, 0:CX]
         to = slice(0, R) if side == 0 else slice(R + CY, 2 * R + CY)
-        ybuf[:, to, :] = near[1 : CZ + 1, :, CX:]
+        ybuf[:, to, :] += near[1 : CZ + 1, :, CX:]
 
     @pl.loop(0, CZ, unroll=2)
     def _(z):
@@ -823,9 +883,10 @@
             vm((V, ANG, DW), BF16),
             vm((V, ANG * DW), BF16),
             vm((2, CHUNK * PITCH, 128), F32),
-            block, block, block,
+            block, block,
             vm((ROWS, CX), F32),
-            block,
+            vm((ROWS, CX), F32),
+            vm((ROWS, CX), F32),
             vm((CZ + 2, CY, CX), F32),
             vm((CZ + 32, CY, CX), F32),
             vm((CZ + 16, CY, CX), F32),
@@ -837,8 +898,11 @@
             vm((ANG, NBLK * DW), F32),
             vm((2, 2, R * CY, CX), BF16),
             vm((2, 2, R * CY, CX), BF16),
-            vm((2, 16 * CY, CX), BF16),
-            vm((2, 16 * CY, CX), BF16),
+            vm((128, V), BF16),
+            vm((128, 128), BF16),
+            vm((CZ, V), F32),
+            vm((CY + 32, CZ, CX), F32),
+            vm((CY + 16, CZ, CX), F32),
             vm((3, 2, CZ * R, CX), BF16),
             vm((3, 2, CZ * R, CX), BF16),
             vm((ROWS, CX), BF16),

time: 76.8 us -> 74.9 us (0.975)
  Pallas kernels: 74.4 us -> 72.5 us
    pallas_call x1, Pallas kernels: 74.4 us -> 72.5 us  [body(): pl.pallas_call(kernel, out_shape=(pltpu.VMEM((CZ, CY, CX), F32), pltpu.VM...]
where the time goes in v7:
time: 74.9 us; the launch traced here: 74.8 us
  Pallas kernels  72.5 us (97%)
  local copies, waits for them, and re-layouts  1.58 us (2%)
    pallas_call x1, Pallas kernels, body(): pl.pallas_call(kernel, out_shape=(pltpu.VMEM((CZ, CY, CX), F32), pltpu.VM...  72.5 us
    unnamed x2, local copies, waits for them, and re-layouts  1.58 us

profile of v7, /device:TPU:1, one launch (start us, length us, event | category | flops | bytes accessed | tf_op | source)
XLA Modules:
  0.0 74.8 jit_solution(185261197944272232)
XLA Ops:
  0.6 72.5 %shard_map.68 = (f32[32,16,128]{2,1,0:T(8,128)S(1)}, f32[3,32,16,128]{3,2,1,0:T(8,128)S(1)}) custom-call(f32[32,16,128]{2,1,0:T(8,128)} %start_ref.1, f32[1,8,1024]{2,1,0:T(8,128)} %meas_ref.1, bf16[2048,8,256]{2,1,0:T(8,128)(2,1)} %tiles_ref.1, s32[4,8,8]{2,1,0:T(8,128)} %tb_ref.1, s32[8]{0:T(128)} %row_ref.1), custom_call_target="tpu_custom_call" | custom-call | tf_op jit(solution)/shard_map/pallas_call | solution.py:868
  73.2 0.7 copy.9
  73.9 0.9 %copy.10 = f32[3,32,16,128]{3,2,1,0:T(8,128)} copy(f32[3,32,16,128]{3,2,1,0:T(8,128)S(1)} %get-tuple-element.3) | data formatting | bytes 1572864

commit v8 on v7

--- a/solution.py
+++ b/solution.py
@@ -31,6 +31,7 @@
 ROWS9P = -(-ROWS9 // 128) * 128
 PITCH = 9
 SPLIT = 4
+TURN = 3
 ORDER_ALL = sorted(
     ((dy, t) for dy in range(GZ) for t in range(GY * GX) if dy or t),
     key=lambda s: -(
@@ -41,6 +42,10 @@
 
 RAW = [math.exp(-k * k / 12.5) for k in range(-R, R + 1)]
 TAPS = [r / sum(RAW) for r in RAW]
+TWICE = [
+    sum(TAPS[k] * TAPS[d + 2 * R - k] for k in range(2 * R + 1) if 0 <= d + 2 * R - k <= 2 * R)
+    for d in range(2 * R + 1)
+]
 
 
 def dot(a, b, dims):
@@ -56,9 +61,9 @@
 def kernel(
     start_ref, meas_ref, tiles_ref, tb_ref, row_ref,
     x_out, dual_out,
-    raw, mat, tmp, x0, w1, w2, res, qbuf, xa, zbuf, zmid, ybuf, ymid, tbv, obs, mis, acc,
-    zs, zr, zst, tz, v1z, umid, ytwo, ys, yr, ys2, yr2, xs, xr,
-    zs9, zr9, ys9, yr9, xs9, xr9,
+    raw, mat, turned, tmp, x0, w1, w2, res, qbuf, xa, zbuf, zmid, ybuf, ymid, tbv, obs, mis, acc,
+    zs, zr, zst, tz, tz9, v1z, umid, ytwo, ys, yr, ys2, yr2, xs, xr,
+    ys9, yr9, xs9, xr9,
     fzs, fzr, fys, fyr, fxs, fxr, fzs2, fzr2, fys2, fyr2, fxs2, fxr2, fz2, fy2,
     stage, sl, snd1, rcv1, snd2, rcv2,
     hterm, back, dl, dlm, xlr, bdl,
@@ -99,6 +104,13 @@
     ]
     for c in ld:
         c.start()
+
+    def turn(low, high):
+        @pl.loop(low, high)
+        def _(c):
+            rows = pl.ds(pl.multiple_of(c * DW, DW), DW)
+            for a in range(ANG):
+                turned[a * DW : (a + 1) * DW, rows] = mat[rows, a * DW : (a + 1) * DW].T
 
     def tile_copy(c):
         rows = pl.ds(c * LOAD, LOAD)
@@ -178,14 +190,17 @@
 
     zhub = [zswap(0, zs.at[0], zr.at[0], None)]
     zhub.append(zswap(1, zs.at[1], zr.at[1], zhub[0]))
-    zhub2 = Hub(
-        [
-            ((-1, 0, 0), zst.at[0:16], zst.at[80:96], z_send.at[0], z_recv.at[0, 0]),
-            ((1, 0, 0), zst.at[16:32], zst.at[64:80], z_send.at[1], z_recv.at[0, 1]),
-        ],
-        zhub[1],
-    )
-    zhub.append(zswap(1, zs9, zr9, zhub2))
+    def zstack(k, before):
+        return Hub(
+            [
+                ((-1, 0, 0), zst.at[0:16], zst.at[80:96], z_send.at[0], z_recv.at[k, 0]),
+                ((1, 0, 0), zst.at[16:32], zst.at[64:80], z_send.at[1], z_recv.at[k, 1]),
+            ],
+            before,
+        )
+
+    zhub2 = zstack(0, zhub[1])
+    zhub.append(zstack(1, None))
 
     def yxswap(n, k, before):
         low, high = yr.at[n, 0], yr.at[n, 1]
@@ -341,7 +356,7 @@
         def _(z):
             out[z] = taps(lambda k: zbuf[z + k])
 
-    def send_yx(n, w):
+    def send_yx(n, w, now=True):
         v = w[...]
         ys[n, 0] = v[:, 0:R, :].reshape(CZ * R, CX).astype(BF16)
         ys[n, 1] = v[:, CY - R :, :].reshape(CZ * R, CX).astype(BF16)
@@ -349,7 +364,8 @@
         f = dot(pick, jnp.concatenate([hi, lo], axis=1), ((1,), (1,))).astype(BF16)
         xs[n, 0] = f[0:16]
         xs[n, 1] = f[16:32]
-        yxhub[n].start()
+        if now:
+            yxhub[n].start()
 
     def rows_of(m, slot, weights):
         halo = xr[m, slot].reshape(32, ROWS)
@@ -542,7 +558,7 @@
                 ].astype(BF16)
         with scope("mm_bwd"):
             for c in range(ANG):
-                put(c, dot(sl[...], mat[c * DW : (c + 1) * DW, :], ((1,), (1,))))
+                put(c, dot(sl[...], turned[:, c * DW : (c + 1) * DW], ((1,), (0,))))
 
     send_z(0, x0)
     send_faces(0, x0)
@@ -611,13 +627,20 @@
     twice = (
         dot(thi, uhi, ((1,), (0,))) + dot(thi, ulo, ((1,), (0,))) + dot(tlo, uhi, ((1,), (0,)))
     )
+    hi, lo = split(gauss(iota((48, CX), 0) - 1 - from_place(iota((48, CX), 1))))
+    tz9[0:48] = hi
+    tz9[48:96] = lo
     once = gauss(iota(shape1, 0) - from_place(iota(shape1, 1)))
     for i, t in enumerate((twice, once)):
         hi, lo = split(t)
         tz[32 * i : 32 * i + 32] = hi
         tz[64 + 32 * i : 96 + 32 * i] = lo
 
+    with scope("turn"):
+        turn(0, TURN)
     return_misfit(0)
+    with scope("turn"):
+        turn(TURN, ANG)
     blur_z(1, x0, w1)
     send_yx(1, w1)
 
@@ -664,13 +687,6 @@
     umid[16:32] += rows_of(3, 1, wx2[...]).reshape(slab)
     for side in range(2):
         umid[32 * side : 32 * side + 16] = rows_of(3, 2 * side, wx2[...]).reshape(slab)
-    with scope("wait_yx2"):
-        yxhub2.wait_recv(slice(6, 8))
-    send_yx(2, w1)
-    for side in range(2):
-        y = yr2[side]
-        rows = dot(jnp.concatenate([y, y], axis=1), bx2[CX:], ((1,), (0,)))
-        umid[32 * side : 32 * side + 16] += rows.reshape(slab)
 
     @pl.loop(0, CY + 16)
     def _(y):
@@ -678,8 +694,23 @@
         ytwo[y] = jnp.where(out, 0.0, taps(lambda k: umid[y + k]))
 
     for y in range(CY):
-        q = qbuf[y * CZ : (y + 1) * CZ, :]
-        v = q - STEP * taps(lambda k: ytwo[y + k])
+        rows = slice(y * CZ, (y + 1) * CZ)
+        qbuf[rows, :] = qbuf[rows, :] - STEP * taps(lambda k: ytwo[y + k])
+    send_yx(2, w1, now=False)
+    with scope("wait_yx2"):
+        yxhub2.wait_recv(slice(6, 8))
+    yxhub[2].start()
+    for side in range(2):
+        y = yr2[side]
+        rows = dot(jnp.concatenate([y, y], axis=1), bx2[CX:], ((1,), (0,)))
+        umid[32 * side : 32 * side + 16] = rows.reshape(slab)
+    for y in range(CY):
+        t = TWICE[16] * (umid[y] + umid[32 + y])
+        for r in range(y + 1, CY):
+            t += TWICE[y + 16 - r] * umid[r]
+        for r in range(y):
+            t += TWICE[16 + r - y] * umid[32 + r]
+        v = qbuf[y * CZ : (y + 1) * CZ, :] - STEP * t
         sl[:, y * CX : (y + 1) * CX] = v.astype(BF16)
 
     project(1)
@@ -723,30 +754,22 @@
         redz_copy(0, t).start()
     send_terms()
 
-    def spread_rows(c, b):
-        for h in range(2):
-            res[pl.ds(2 * c + h, CZ, stride=CY), :] = b[:, h * 128 : (h + 1) * 128]
-
-    backproject(1, spread_rows)
-    zs9[0] = res[0 : (R + 1) * CY].astype(BF16)
-    zs9[1] = res[(CZ - R - 1) * CY :].astype(BF16)
+    zhub2.wait_send()
+    backproject(1, to_stack)
     zhub[2].start()
     forward_sums(0)
-    zbuf[R + 1 : R + 1 + CZ] = res[...].reshape(CZ, CY, CX)
     with scope("wait_z"):
         zhub[2].wait_recv()
-    zbuf[0 : R + 1] = zr9[0].astype(F32).reshape(R + 1, CY, CX)
-    zbuf[R + 1 + CZ : 2 * R + 2 + CZ] = zr9[1].astype(F32).reshape(R + 1, CY, CX)
-
-    @pl.loop(0, CZ + 2, unroll=2)
-    def _(z):
-        zmid[z] = taps(lambda k: zbuf[z + k])
-
-    outer = zmid[0 : CZ + 2]
+    for c in range(ANG):
+        o = dot(tz9[...], zst[:, c * DW : (c + 1) * DW], ((1,), (0,)))
+        o = o[0:40] + o[48:88]
+        for h in range(2):
+            zmid[pl.ds(2 * c + h, 40, stride=CY), :] = o[:, h * 128 : (h + 1) * 128]
+    outer = zmid[0:ROWS9].reshape(CZ + 2, CY, CX)
     n9 = (CZ + 2) * R
     for side, at, ninth in ((0, slice(0, R), R), (1, slice(CY - R, CY), CY - R - 1)):
         ys9[side, 0:n9] = outer[:, at, :].reshape(n9, CX).astype(BF16)
-        ys9[side, n9:] = outer[1 : CZ + 1, ninth, :].astype(BF16)
+        ys9[side, n9:] = zmid[pl.ds(CY + ninth, CZ, stride=CY), :].astype(BF16)
     hi, lo = split(outer.reshape(ROWS9, CX))
     f = dot(pick2, hi, ((1,), (1,))).astype(BF16)
     xs9[0, :, 0:ROWS9] = f[0:16]
@@ -804,7 +827,7 @@
         near = rows[0:n9].reshape(CZ + 2, R, 2 * CX)
         to = slice(16 - R, 16) if side == 0 else slice(16 + CY, 16 + CY + R)
         ymid[0 : CZ + 2, to, :] += near[:, :, 0:CX]
-        ymid[1 : CZ + 1, (15 - R if side == 0 else 16 + CY + R), :] += rows[n9:, 0:CX]
+        fy2[side] = fy2[side] - STEP * TAPS[0] * rows[n9:, 0:CX]
         to = slice(0, R) if side == 0 else slice(R + CY, 2 * R + CY)
         ybuf[:, to, :] += near[1 : CZ + 1, :, CX:]
 
@@ -882,6 +905,7 @@
         scratch_shapes=[
             vm((V, ANG, DW), BF16),
             vm((V, ANG * DW), BF16),
+            vm((ANG * DW, V), BF16),
             vm((2, CHUNK * PITCH, 128), F32),
             block, block,
             vm((ROWS, CX), F32),
@@ -889,7 +913,7 @@
             vm((ROWS, CX), F32),
             vm((CZ + 2, CY, CX), F32),
             vm((CZ + 32, CY, CX), F32),
-            vm((CZ + 16, CY, CX), F32),
+            vm((40 * CY, CX), F32),
             vm((CZ, CY + 16, CX), F32),
             vm((CZ + 2, CY + 32, CX), F32),
             vm((BRICKS, ANG, CX), F32),
@@ -900,6 +924,7 @@
             vm((2, 2, R * CY, CX), BF16),
             vm((128, V), BF16),
             vm((128, 128), BF16),
+            vm((96, 128), BF16),
             vm((CZ, V), F32),
             vm((CY + 32, CZ, CX), F32),
             vm((CY + 16, CZ, CX), F32),
@@ -909,8 +934,6 @@
             vm((2, ROWS, CX), BF16),
             vm((4, 2, 16, ROWS), BF16),
             vm((4, 3, 2, 16, ROWS), BF16),
-            vm((2, (R + 1) * CY, CX), BF16),
-            vm((2, (R + 1) * CY, CX), BF16),
             vm((2, (CZ + 2) * R + CZ, CX), BF16),
             vm((2, (CZ + 2) * R + CZ, CX), BF16),
             vm((2, 16, ROWS9P), BF16),

time: 74.9 us -> 72.9 us (0.973)
  Pallas kernels: 72.5 us -> 70.5 us
    pallas_call x1, Pallas kernels: 72.5 us -> 70.5 us  [body(): pl.pallas_call(kernel, out_shape=(pltpu.VMEM((CZ, CY, CX), F32), pltpu.VM...]
where the time goes in v8:
time: 72.9 us; the launch traced here: 72.7 us
  Pallas kernels  70.5 us (97%)
  local copies, waits for them, and re-layouts  1.58 us (2%)
    pallas_call x1, Pallas kernels, body(): pl.pallas_call(kernel, out_shape=(pltpu.VMEM((CZ, CY, CX), F32), pltpu.VM...  70.5 us
    unnamed x2, local copies, waits for them, and re-layouts  1.58 us

profile of v8, /device:TPU:1, one launch (start us, length us, event | category | flops | bytes accessed | tf_op | source)
XLA Modules:
  0.0 72.7 jit_solution(1276970595849147761)
XLA Ops:
  0.6 70.5 %shard_map.68 = (f32[32,16,128]{2,1,0:T(8,128)S(1)}, f32[3,32,16,128]{3,2,1,0:T(8,128)S(1)}) custom-call(f32[32,16,128]{2,1,0:T(8,128)} %start_ref.1, f32[1,8,1024]{2,1,0:T(8,128)} %meas_ref.1, bf16[2048,8,256]{2,1,0:T(8,128)(2,1)} %tiles_ref.1, s32[4,8,8]{2,1,0:T(8,128)} %tb_ref.1, s32[8]{0:T(128)} %row_ref.1), custom_call_target="tpu_custom_call" | custom-call | tf_op jit(solution)/shard_map/pallas_call | solution.py:891
  71.1 0.7 copy.9
  71.8 0.9 %copy.10 = f32[3,32,16,128]{3,2,1,0:T(8,128)} copy(f32[3,32,16,128]{3,2,1,0:T(8,128)S(1)} %get-tuple-element.3) | data formatting | bytes 1572864

commit v9 on v8

--- a/solution.py
+++ b/solution.py
@@ -70,7 +70,7 @@
     red0, redz, red1, redx, redall,
     bx, wx, bx2, wx2, bx9, wx9,
     load_sem, tile_sem, z_send, z_recv, yx_send, yx_recv, f_send, f_recv,
-    a_send, a_recv, rz_send, rz_recv, rx_send, rx_recv, all_send, all_recv,
+    a_send, a_recv, rz_send, rz_recv, rx_send, rx_recv, all_send, all_recv, meet,
 ):
     gz, gy, gx = lax.axis_index("gz"), lax.axis_index("gy"), lax.axis_index("gx")
     me = gy * GX + gx
@@ -89,14 +89,34 @@
         x = 2 * z + lax.rem(x, 2)
         return y * GX + x, (gz, y, x)
 
-    for t in range(1, BRICKS):
-        pl.semaphore_signal(barrier, inc=1, device_id=member(t)[1], device_id_type=MESH)
-
-    @pl.loop(1, GZ)
-    def _(t):
-        pl.semaphore_signal(
-            barrier, inc=1, device_id=(lax.rem(gz + t, GZ), gy, gx), device_id_type=MESH
-        )
+    def there(dz, dy, dx):
+        ok = True
+        for d, at, n in ((dz, gz, GZ), (dy, gy, GY), (dx, gx, GX)):
+            if d:
+                near = at >= -d if d < 0 else at < n - d
+                ok = near if ok is True else jnp.logical_and(ok, near)
+        return ok
+
+    def greet(sem, stride):
+        steps = (-stride, 0, stride)
+        places = [(0, dy, dx) for dy in steps for dx in steps if dy or dx]
+        places += [(-stride, 0, 0), (stride, 0, 0)]
+        if stride == 4:
+            places = [(0, 0, -stride), (0, 0, stride)]
+        heard = 0
+        for dz, dy, dx in places:
+            ok = there(dz, dy, dx)
+            heard = heard + ok.astype(jnp.int32)
+
+            @pl.when(ok)
+            def _():
+                pl.semaphore_signal(
+                    sem, inc=1, device_id=(gz + dz, gy + dy, gx + dx), device_id_type=MESH
+                )
+
+        return lambda: pl.semaphore_wait(sem, heard)
+
+    wait_near = greet(barrier, 1)
 
     ld = [
         pltpu.make_async_copy(start_ref, x0, load_sem.at[0]),
@@ -116,14 +136,6 @@
         rows = pl.ds(c * LOAD, LOAD)
         return pltpu.make_async_copy(tiles_ref.at[rows], raw.at[rows], tile_sem.at[c])
 
-
-    def there(dz, dy, dx):
-        ok = True
-        for d, at, n in ((dz, gz, GZ), (dy, gy, GY), (dx, gx, GX)):
-            if d:
-                near = at > 0 if d < 0 else at < n - 1
-                ok = near if ok is True else jnp.logical_and(ok, near)
-        return ok
 
     class Hub:
         def __init__(self, items, before=None):
@@ -306,8 +318,13 @@
     for a in range(ANG):
         acc[pl.ds(a, 1), :] = obs[0, pl.ds(row_ref[a], 1), :]
 
+    def stage_z(n, src):
+        zs[n, 0] = src[0:R].reshape(R * CY, CX).astype(BF16)
+        zs[n, 1] = src[CZ - R : CZ].reshape(R * CY, CX).astype(BF16)
+
+    stage_z(0, x0)
     with scope("wait_barrier"):
-        pl.semaphore_wait(barrier, BRICKS - 1 + GZ - 1)
+        wait_near()
 
     def send_faces(n, src):
         fzs[n, 0] = src[0]
@@ -333,11 +350,6 @@
             fxs2[0, i] = f[0:16]
             fxs2[1, i] = f[16:32]
         fhub[2].start()
-
-    def send_z(n, src):
-        zs[n, 0] = src[0:R].reshape(R * CY, CX).astype(BF16)
-        zs[n, 1] = src[CZ - R : CZ].reshape(R * CY, CX).astype(BF16)
-        zhub[n].start()
 
     def taps(at):
         t = TAPS[R] * at(R)
@@ -505,6 +517,8 @@
 
         if n:
             sent(0, snd2)
+        else:
+            wait_round()
         for t in range(1, BRICKS):
             d, dev = member(t)
             snd1[n, d] = block_of(d)
@@ -560,16 +574,21 @@
             for c in range(ANG):
                 put(c, dot(sl[...], turned[:, c * DW : (c + 1) * DW], ((1,), (0,))))
 
-    send_z(0, x0)
+    zhub[0].start()
+    wait_round = greet(meet.at[0], 1)
     send_faces(0, x0)
     relayout(0, SPLIT)
     blur_z(0, x0, w1)
     send_yx(0, w1)
+    wait_round()
+    wait_round = greet(meet.at[1], 2)
     relayout(SPLIT, NCHUNK)
 
     def to_res(z, v):
         res[pl.ds(pl.multiple_of(z * CY, CY), CY), :] = v
 
+    wait_round()
+    wait_round = greet(meet.at[2], 4)
     blur_yx(0, w1, to_res)
     for y in range(CY):
         sl[:, y * CX : (y + 1) * CX] = res[pl.ds(y, CZ, stride=CY), :].astype(BF16)
@@ -592,7 +611,8 @@
         x0[z] = xa[z + 1] - h
         back[z] = shrunk
 
-    send_z(1, x0)
+    stage_z(1, x0)
+    zhub[1].start()
 
     shape1, shape2 = (160, 256), (256, CX)
     i, m = iota(shape1, 0), iota(shape1, 1) - 8
@@ -989,6 +1009,7 @@
             dma,
             dma,
             dma,
+            pltpu.SemaphoreType.REGULAR((3,)),
         ],
         compiler_params=pltpu.CompilerParams(
             collective_id=0, has_side_effects=True, vmem_limit_bytes=60 * 1024 * 1024

time: 72.9 us -> 71.6 us (0.982)
  Pallas kernels: 70.5 us -> 69.2 us
    pallas_call x1, Pallas kernels: 70.5 us -> 69.2 us  [body(): pl.pallas_call(kernel, out_shape=(pltpu.VMEM((CZ, CY, CX), F32), pltpu.VM...]
where the time goes in v9:
time: 71.6 us; the launch traced here: 71.4 us
  Pallas kernels  69.2 us (97%)
  local copies, waits for them, and re-layouts  1.58 us (2%)
    pallas_call x1, Pallas kernels, body(): pl.pallas_call(kernel, out_shape=(pltpu.VMEM((CZ, CY, CX), F32), pltpu.VM...  69.2 us
    unnamed x2, local copies, waits for them, and re-layouts  1.58 us

profile of v9, /device:TPU:1, one launch (start us, length us, event | category | flops | bytes accessed | tf_op | source)
XLA Modules:
  0.0 71.4 jit_solution(16052827798259890651)
XLA Ops:
  0.6 69.2 %shard_map.68 = (f32[32,16,128]{2,1,0:T(8,128)S(1)}, f32[3,32,16,128]{3,2,1,0:T(8,128)S(1)}) custom-call(f32[32,16,128]{2,1,0:T(8,128)} %start_ref.1, f32[1,8,1024]{2,1,0:T(8,128)} %meas_ref.1, bf16[2048,8,256]{2,1,0:T(8,128)(2,1)} %tiles_ref.1, s32[4,8,8]{2,1,0:T(8,128)} %tb_ref.1, s32[8]{0:T(128)} %row_ref.1), custom_call_target="tpu_custom_call" | custom-call | tf_op jit(solution)/shard_map/pallas_call | solution.py:911
  69.8 0.7 copy.9
  70.5 0.9 %copy.10 = f32[3,32,16,128]{3,2,1,0:T(8,128)} copy(f32[3,32,16,128]{3,2,1,0:T(8,128)S(1)} %get-tuple-element.3) | data formatting | bytes 1572864

commit v10 on v9

--- a/solution.py
+++ b/solution.py
@@ -31,6 +31,7 @@
 ROWS9P = -(-ROWS9 // 128) * 128
 PITCH = 9
 SPLIT = 4
+NEAR = 16
 TURN = 3
 ORDER_ALL = sorted(
     ((dy, t) for dy in range(GZ) for t in range(GY * GX) if dy or t),
@@ -70,7 +71,7 @@
     red0, redz, red1, redx, redall,
     bx, wx, bx2, wx2, bx9, wx9,
     load_sem, tile_sem, z_send, z_recv, yx_send, yx_recv, f_send, f_recv,
-    a_send, a_recv, rz_send, rz_recv, rx_send, rx_recv, all_send, all_recv, meet,
+    a_send, a_recv, rz_send, rz_recv, rx_send, rx_recv, all_send, all_recv, meet, near_recv,
 ):
     gz, gy, gx = lax.axis_index("gz"), lax.axis_index("gy"), lax.axis_index("gx")
     me = gy * GX + gx
@@ -522,23 +523,41 @@
         for t in range(1, BRICKS):
             d, dev = member(t)
             snd1[n, d] = block_of(d)
-            send_block(n, 0, snd1, rcv1, d, dev)
-
-        rcv1[n, me] = block_of(me)
+            pltpu.make_async_remote_copy(
+                snd1.at[n, d], rcv1.at[n, t], a_send,
+                a_recv.at[n, 0] if t < NEAR else near_recv.at[n],
+                device_id=dev, device_id_type=MESH,
+            ).start()
+
+        rcv1[n, 0] = block_of(me)
 
     def return_misfit(n):
+        def sender(t):
+            if t == 0:
+                return me
+            dx, dz, dc = ORDER[t - 1]
+            x = lax.rem(chip_x + 4 - dx, 4)
+            z = lax.rem(chip_z + 4 - dz, 4)
+            y = 2 * (x // 2) + lax.rem(core + dc, 2)
+            return y * GX + 2 * z + lax.rem(x, 2)
+
+        def add(slots, sums):
+            for t in slots:
+                x = rcv1[n, t].astype(F32)
+                b = tbv[sender(t)]
+                b = jnp.concatenate([b, b], axis=1)
+                sums = [sums[q] + jnp.where(b == float(q), x, 0.0) for q in range(NBLK)]
+            return sums
+
         with scope("wait_a1"):
-            arrivals(rcv1.at[n], a_recv.at[n, 0])
-
-        def add(s, sums):
-            x = rcv1[n, s].astype(F32)
-            t = tbv[s]
-            t = jnp.concatenate([t, t], axis=1)
-            return tuple(sums[q] + jnp.where(t == float(q), x, 0.0) for q in range(NBLK))
-
-        sums = lax.fori_loop(
-            0, BRICKS, add, tuple(jnp.zeros((ANG, DW), F32) for _ in range(NBLK)), unroll=2
-        )
+            got = rcv1.at[n, pl.ds(NEAR, BRICKS - NEAR)]
+            pltpu.make_async_copy(got, got, near_recv.at[n]).wait()
+        sums = [jnp.zeros((ANG, DW), F32) for _ in range(NBLK)]
+        sums = add([0, *range(NEAR, BRICKS)], sums)
+        with scope("wait_a1"):
+            got = rcv1.at[n, pl.ds(1, NEAR - 1)]
+            pltpu.make_async_copy(got, got, a_recv.at[n, 0]).wait()
+        sums = add(range(1, NEAR), sums)
         for q in range(NBLK):
             cols = slice(q * DW, (q + 1) * DW)
             mis[:, cols] = (sums[q] - acc[:, cols]).astype(BF16).astype(F32)
@@ -1010,6 +1029,7 @@
             dma,
             dma,
             pltpu.SemaphoreType.REGULAR((3,)),
+            dma((2,)),
         ],
         compiler_params=pltpu.CompilerParams(
             collective_id=0, has_side_effects=True, vmem_limit_bytes=60 * 1024 * 1024

time: 71.6 us -> 71.5 us (level)
  no operation moved by 1% of the time
where the time goes in v10:
time: 71.5 us; the launch traced here: 71.3 us
  Pallas kernels  69.1 us (97%)
  local copies, waits for them, and re-layouts  1.58 us (2%)
    pallas_call x1, Pallas kernels, body(): pl.pallas_call(kernel, out_shape=(pltpu.VMEM((CZ, CY, CX), F32), pltpu.VM...  69.1 us
    unnamed x2, local copies, waits for them, and re-layouts  1.58 us

profile of v10, /device:TPU:1, one launch (start us, length us, event | category | flops | bytes accessed | tf_op | source)
XLA Modules:
  0.0 71.3 jit_solution(3978650234667322294)
XLA Ops:
  0.6 69.1 %shard_map.68 = (f32[32,16,128]{2,1,0:T(8,128)S(1)}, f32[3,32,16,128]{3,2,1,0:T(8,128)S(1)}) custom-call(f32[32,16,128]{2,1,0:T(8,128)} %start_ref.1, f32[1,8,1024]{2,1,0:T(8,128)} %meas_ref.1, bf16[2048,8,256]{2,1,0:T(8,128)(2,1)} %tiles_ref.1, s32[4,8,8]{2,1,0:T(8,128)} %tb_ref.1, s32[8]{0:T(128)} %row_ref.1), custom_call_target="tpu_custom_call" | custom-call | tf_op jit(solution)/shard_map/pallas_call | solution.py:930
  69.7 0.7 copy.9
  70.4 0.9 %copy.10 = f32[3,32,16,128]{3,2,1,0:T(8,128)} copy(f32[3,32,16,128]{3,2,1,0:T(8,128)S(1)} %get-tuple-element.3) | data formatting | bytes 1572864
